TPU v7x, 16 devices: a whole 2x2x2 slice. The times are simulated.
16 devices in a mesh: dp: 16 (over z, y, x, core).
Axes of the slice: x: 2, y: 2, z: 2, core: 2. Of those that a mesh axis runs over, the one named last changes fastest.
Arguments:
- x_saved: bfloat16 [32, 768, 1536], P('dp')
- grad_out: bfloat16 [32, 768, 1536], P('dp')
- positions: int32 [32, 768], P('dp')
- attn_gain: bfloat16 [1536], replicated
- w_query: bfloat16 [1536, 12, 128], replicated
- w_key: bfloat16 [1536, 2, 128], replicated
- w_value: bfloat16 [1536, 2, 128], replicated
- w_out: bfloat16 [12, 128, 1536], replicated
- mlp_gain: bfloat16 [1536], replicated
- w_gate: bfloat16 [1536, 8960], replicated
- w_up: bfloat16 [1536, 8960], replicated
- w_down: bfloat16 [8960, 1536], replicated
- master_flat: float32 [46795776], P('dp')
- adam_mean: float32 [46795776], P('dp')
- adam_var: float32 [46795776], P('dp')
Outputs:
- output 1: bfloat16 [32, 768, 1536], P('dp')
- output 2: bfloat16 [1536], replicated
- output 3: bfloat16 [1536, 12, 128], replicated
- output 4: bfloat16 [1536, 2, 128], replicated
- output 5: bfloat16 [1536, 2, 128], replicated
- output 6: bfloat16 [12, 128, 1536], replicated
- output 7: bfloat16 [1536], replicated
- output 8: bfloat16 [1536, 8960], replicated
- output 9: bfloat16 [1536, 8960], replicated
- output 10: bfloat16 [8960, 1536], replicated
- output 11: float32 [46795776], P('dp')
- output 12: float32 [46795776], P('dp')
- output 13: float32 [46795776], P('dp')
- output 14: float32 [], replicated
All inputs are finite; a program needn't handle non-finite values.
Results may differ from a plain program's by a relative error of at most 0.0134382.
Values are sent between devices in bfloat16 or wider.
A program may use at most 1.25 GiB of HBM per device.

v0:
```python
import jax
import jax.numpy as jnp
from jax import lax
from jax.sharding import PartitionSpec as P

NORM_EPS = 1e-5
ROPE_BASE = 10000.0
LEARN_RATE = 2e-3
BETA_ONE = 0.9
BETA_TWO = 0.95
ADAM_EPS = 1e-8
WEIGHT_DECAY = 0.1
STEP_COUNT = 100


def rope_tables(positions, head_dim):
    half_dim = head_dim // 2
    inv_freq = ROPE_BASE ** (-2.0 * jnp.arange(half_dim, dtype=jnp.float32) / head_dim)
    angles = positions.astype(jnp.float32)[:, :, None] * inv_freq
    cos_full = jnp.concatenate([jnp.cos(angles), jnp.cos(angles)], axis=-1)[:, :, None, :]
    sin_full = jnp.concatenate([jnp.sin(angles), jnp.sin(angles)], axis=-1)[:, :, None, :]
    return cos_full, sin_full


def rope_apply(values, cos_full, sin_full):
    half_dim = values.shape[-1] // 2
    rotated = jnp.concatenate([-values[..., half_dim:], values[..., :half_dim]], axis=-1)
    return values * cos_full + rotated * sin_full


def rope_back(grad_rot, cos_full, sin_full):
    half_dim = grad_rot.shape[-1] // 2
    scaled = grad_rot * sin_full
    return grad_rot * cos_full + jnp.concatenate([scaled[..., half_dim:], -scaled[..., :half_dim]], axis=-1)


def rms_parts(values):
    inv_rms = lax.rsqrt(jnp.mean(values * values, axis=-1, keepdims=True) + NORM_EPS)
    return inv_rms, values * inv_rms


def rms_back(d_normed, gain_wide, inv_rms, x_hat):
    d_hat = d_normed * gain_wide
    return inv_rms * (d_hat - x_hat * jnp.mean(d_hat * x_hat, axis=-1, keepdims=True))


def local_grads(x_loc, dy_loc, pos_loc, w_list):
    attn_gain, w_query, w_key, w_value, w_out, mlp_gain, w_gate, w_up, w_down = w_list
    num_seqs, seq_len, model_dim = x_loc.shape
    num_heads, head_dim = w_query.shape[1], w_query.shape[2]
    kv_heads = w_key.shape[1]
    group_size = num_heads // kv_heads
    n_tok = num_seqs * seq_len
    wq_flat = w_query.reshape(model_dim, num_heads * head_dim)
    wk_flat = w_key.reshape(model_dim, kv_heads * head_dim)
    wv_flat = w_value.reshape(model_dim, kv_heads * head_dim)
    wo_flat = w_out.reshape(num_heads * head_dim, model_dim)
    dy_flat = dy_loc.reshape(n_tok, model_dim)
    x_wide = x_loc.reshape(n_tok, model_dim).astype(jnp.float32)
    inv_one, value_a8 = rms_parts(x_wide)
    gain_one = attn_gain.astype(jnp.float32)
    normed = (value_a8 * gain_one).astype(jnp.bfloat16)
    q_pre = jnp.dot(normed, wq_flat, preferred_element_type=jnp.float32).reshape(num_seqs, seq_len, num_heads, head_dim)
    k_pre = jnp.dot(normed, wk_flat, preferred_element_type=jnp.float32).reshape(num_seqs, seq_len, kv_heads, head_dim)
    v_heads = jnp.dot(normed, wv_flat, preferred_element_type=jnp.float32).astype(jnp.bfloat16).reshape(num_seqs, seq_len, kv_heads, head_dim)
    cos_full, sin_full = rope_tables(pos_loc, head_dim)
    q_rot = rope_apply(q_pre, cos_full, sin_full).astype(jnp.bfloat16).reshape(num_seqs, seq_len, kv_heads, group_size, head_dim)
    k_rot = rope_apply(k_pre, cos_full, sin_full).astype(jnp.bfloat16)
    score_scale = head_dim ** -0.5
    scores = jnp.einsum('bqkgd,bskd->bkgqs', q_rot, k_rot, preferred_element_type=jnp.float32) * score_scale
    causal = lax.iota(jnp.int32, seq_len)[:, None] >= lax.iota(jnp.int32, seq_len)[None, :]
    attn_probs = jax.nn.softmax(jnp.where(causal, scores, -1e30), axis=-1)
    probs_low = attn_probs.astype(jnp.bfloat16)
    context = jnp.einsum('bkgqs,bskd->bqkgd', probs_low, v_heads, preferred_element_type=jnp.float32).astype(jnp.bfloat16)
    context = context.reshape(n_tok, num_heads * head_dim)
    attn_out = jnp.dot(context, wo_flat, preferred_element_type=jnp.float32)
    hidden = (x_wide + attn_out).astype(jnp.bfloat16)
    inv_two, array_b8 = rms_parts(hidden.astype(jnp.float32))
    gain_two = mlp_gain.astype(jnp.float32)
    normed_mlp = (array_b8 * gain_two).astype(jnp.bfloat16)
    gate_pre = jnp.dot(normed_mlp, w_gate, preferred_element_type=jnp.float32)
    up_pre = jnp.dot(normed_mlp, w_up, preferred_element_type=jnp.float32)
    gate_sig = jax.nn.sigmoid(gate_pre)
    gate_act = gate_pre * gate_sig
    gated_act = (gate_act * up_pre).astype(jnp.bfloat16)
    g_down = jnp.einsum('nf,nd->fd', gated_act, dy_flat, preferred_element_type=jnp.float32)
    d_gated = jnp.einsum('nd,fd->nf', dy_flat, w_down, preferred_element_type=jnp.float32)
    d_up = (d_gated * gate_act).astype(jnp.bfloat16)
    d_gate = (d_gated * up_pre * gate_sig * (1.0 + gate_pre * (1.0 - gate_sig))).astype(jnp.bfloat16)
    g_gate = jnp.einsum('nd,nf->df', normed_mlp, d_gate, preferred_element_type=jnp.float32)
    g_up = jnp.einsum('nd,nf->df', normed_mlp, d_up, preferred_element_type=jnp.float32)
    d_normed_mlp = (jnp.einsum('nf,df->nd', d_gate, w_gate, preferred_element_type=jnp.float32)
                    + jnp.einsum('nf,df->nd', d_up, w_up, preferred_element_type=jnp.float32))
    g_mlp_gain = jnp.sum(d_normed_mlp * array_b8, axis=0)
    d_hidden = rms_back(d_normed_mlp, gain_two, inv_two, array_b8) + dy_flat.astype(jnp.float32)
    d_hidden_low = d_hidden.astype(jnp.bfloat16)
    g_out = jnp.einsum('nc,nd->cd', context, d_hidden_low, preferred_element_type=jnp.float32)
    d_context = jnp.einsum('nd,cd->nc', d_hidden_low, wo_flat, preferred_element_type=jnp.float32).astype(jnp.bfloat16)
    d_context = d_context.reshape(num_seqs, seq_len, kv_heads, group_size, head_dim)
    d_probs = jnp.einsum('bqkgd,bskd->bkgqs', d_context, v_heads, preferred_element_type=jnp.float32)
    g_values = jnp.einsum('bkgqs,bqkgd->bskd', probs_low, d_context, preferred_element_type=jnp.float32)
    d_scores = (attn_probs * (d_probs - jnp.sum(d_probs * attn_probs, axis=-1, keepdims=True)) * score_scale).astype(jnp.bfloat16)
    d_q_rot = jnp.einsum('bkgqs,bskd->bqkgd', d_scores, k_rot, preferred_element_type=jnp.float32).reshape(num_seqs, seq_len, num_heads, head_dim)
    d_k_rot = jnp.einsum('bkgqs,bqkgd->bskd', d_scores, q_rot, preferred_element_type=jnp.float32)
    d_q_pre = rope_back(d_q_rot, cos_full, sin_full).astype(jnp.bfloat16).reshape(n_tok, num_heads * head_dim)
    d_k_pre = rope_back(d_k_rot, cos_full, sin_full).astype(jnp.bfloat16).reshape(n_tok, kv_heads * head_dim)
    d_v_pre = g_values.astype(jnp.bfloat16).reshape(n_tok, kv_heads * head_dim)
    g_query = jnp.einsum('nd,nc->dc', normed, d_q_pre, preferred_element_type=jnp.float32)
    g_key = jnp.einsum('nd,nc->dc', normed, d_k_pre, preferred_element_type=jnp.float32)
    g_value = jnp.einsum('nd,nc->dc', normed, d_v_pre, preferred_element_type=jnp.float32)
    d_normed = (jnp.einsum('nc,dc->nd', d_q_pre, wq_flat, preferred_element_type=jnp.float32)
                + jnp.einsum('nc,dc->nd', d_k_pre, wk_flat, preferred_element_type=jnp.float32)
                + jnp.einsum('nc,dc->nd', d_v_pre, wv_flat, preferred_element_type=jnp.float32))
    g_attn_gain = jnp.sum(d_normed * value_a8, axis=0)
    d_x = rms_back(d_normed, gain_one, inv_one, value_a8) + d_hidden
    grad_list = [g_attn_gain, g_query, g_key, g_value, g_out, g_mlp_gain, g_gate, g_up, g_down]
    flat_grad = jnp.concatenate([w_grad.astype(jnp.bfloat16).reshape(-1) for w_grad in grad_list])
    return d_x.astype(jnp.bfloat16).reshape(num_seqs, seq_len, model_dim), flat_grad


def gain_offset(w_list):
    return w_list[0].shape[0] + w_list[1].size + w_list[2].size + w_list[3].size + w_list[4].size


def adamw_apply(grad_vec, grad_norm, master_vec, mean_vec, var_vec, first_index, model_dim, gain_two):
    clip_scale = jnp.minimum(1.0, 1.0 / (grad_norm + 1e-6))
    clipped = grad_vec * clip_scale
    new_mean = BETA_ONE * mean_vec + (1.0 - BETA_ONE) * clipped
    new_var = BETA_TWO * var_vec + (1.0 - BETA_TWO) * clipped * clipped
    mean_hat = new_mean / (1.0 - BETA_ONE ** STEP_COUNT)
    var_hat = new_var / (1.0 - BETA_TWO ** STEP_COUNT)
    flat_index = first_index + lax.iota(jnp.int32, master_vec.shape[0])
    is_gain = (flat_index < model_dim) | ((flat_index >= gain_two) & (flat_index < gain_two + model_dim))
    decays = jnp.where(is_gain, 0.0, WEIGHT_DECAY)
    new_master = master_vec - LEARN_RATE * (mean_hat / (jnp.sqrt(var_hat) + ADAM_EPS) + decays * master_vec)
    return new_master, new_mean, new_var


def split_flat(flat_vec, w_list):
    pieces = []
    offset = 0
    for weight in w_list:
        pieces.append(flat_vec[offset:offset + weight.size].reshape(weight.shape))
        offset += weight.size
    return pieces


def solution(mesh):
    dp_size = mesh.shape['dp']

    def per_device(x_loc, dy_loc, pos_loc, attn_gain, w_query, w_key, w_value, w_out, mlp_gain, w_gate, w_up, w_down, master_loc, mean_loc, var_loc):
        w_list = (attn_gain, w_query, w_key, w_value, w_out, mlp_gain, w_gate, w_up, w_down)
        grad_x, flat_grad = local_grads(x_loc, dy_loc, pos_loc, w_list)
        grad_shard = lax.psum_scatter(flat_grad, 'dp', scatter_dimension=0, tiled=True).astype(jnp.float32) / dp_size
        grad_norm = jnp.sqrt(lax.psum(jnp.sum(grad_shard * grad_shard), 'dp'))
        shard_len = master_loc.shape[0]
        shard_start = lax.axis_index('dp') * shard_len
        new_master, new_mean, new_var = adamw_apply(grad_shard, grad_norm, master_loc, mean_loc, var_loc, shard_start, attn_gain.shape[0], gain_offset(w_list))
        gathered = lax.all_gather(new_master.astype(jnp.bfloat16), 'dp', tiled=True)
        new_weights = split_flat(gathered, w_list)
        return (grad_x,) + tuple(new_weights) + (new_master, new_mean, new_var, grad_norm)

    in_specs = (P('dp'),) * 3 + (P(),) * 9 + (P('dp'),) * 3
    out_specs = (P('dp'),) + (P(),) * 9 + (P('dp'),) * 3 + (P(),)
    return jax.shard_map(per_device, mesh=mesh, in_specs=in_specs, out_specs=out_specs, check_vma=False)
```

profile of v0, /device:TPU:0, one launch (start us, length us, event | category | flops | bytes accessed | tf_op | source)
XLA Modules:
  0.0 3351.8 jit_solution(4362198149214914121)
XLA Ops:
  128.3 52.1 %fusion.103 = f32[1536,8960]{1,0:T(8,128)} fusion(bf16[1536,8960]{1,0:T(8,128)(2,1)} %param.24, bf16[1536,1536]{1,0:T(8,128)(2,1)S(1)} %get-tuple-element.74, f32[1536]{0:T(1024)S(1)} %copy-done.28, f32[1536]{0:T(1024)S(1)} %add_rsqrt_fusion), kind=kOutput, calls=%fused_computation.152 | convolution fusion | flops 42288021504 | bytes 87306240 | tf_op jit(solution)/shard_map/dot_general | solution.py:81
  180.4 50.7 %fusion.105 = f32[1536,8960]{1,0:T(8,128)} fusion(bf16[1536,8960]{1,0:T(8,128)(2,1)} %param.25, bf16[1536,1536]{1,0:T(8,128)(2,1)S(1)} %get-tuple-element.74, f32[1536]{0:T(1024)S(1)} %copy-done.28, f32[1536]{0:T(1024)S(1)} %add_rsqrt_fusion), kind=kOutput, calls=%fused_computation.153 | convolution fusion | flops 42288021504 | bytes 87306240 | tf_op jit(solution)/shard_map/dot_general | solution.py:82
  231.0 56.2 %convolution_convert_fusion = bf16[8960,1536]{1,0:T(8,128)(2,1)} fusion(bf16[1536,1536]{1,0:T(8,128)(2,1)} %bitcast.197, f32[1536,8960]{1,0:T(8,128)} %fusion.105, f32[1536,8960]{1,0:T(8,128)} %fusion.103), kind=kOutput, calls=%fused_computation.15 | convolution fusion | flops 42374922240 | bytes 142344192 | tf_op jit(solution)/shard_map/nf,nd->fd/dot_general | solution.py:86
  287.2 75.4 %multiply_convert_fusion.1 = (bf16[1536,8960]{1,0:T(8,128)(2,1)}, bf16[1536,8960]{1,0:T(8,128)(2,1)}) fusion(f32[1536,8960]{1,0:T(8,128)} %fusion.103, f32[1536,8960]{1,0:T(8,128)} %fusion.105, bf16[1536,1536]{1,0:T(8,128)(2,1)} %bitcast.198, bf16[8960,1536]{1,0:T(8,128)(2,1)} %param.26), kind=kOutput, calls=%fused_computation.10 | convolution fusion | flops 42457497600 | bytes 197394432 | tf_op jit(solution)/shard_map/nd,fd->nf/dot_general | solution.py:87
  362.6 52.4 %fusion.117 = f32[1536,1536]{1,0:T(8,128)} fusion(bf16[1536,8960]{1,0:T(8,128)(2,1)} %get-tuple-element.51, bf16[1536,8960]{1,0:T(8,128)(2,1)} %param.24), kind=kOutput, calls=%fused_computation.162 | convolution fusion | flops 42278584320 | bytes 64487424 | tf_op jit(solution)/shard_map/nf,df->nd/dot_general | solution.py:92
  415.0 51.4 %convolution_convert_fusion.2 = bf16[1536,8960]{1,0:T(8,128)(2,1)} fusion(bf16[1536,8960]{1,0:T(8,128)(2,1)} %get-tuple-element.51, bf16[1536,1536]{1,0:T(8,128)(2,1)S(1)} %copy-done.7, f32[1536]{0:T(1024)S(1)} %copy-done.29, f32[1536]{0:T(1024)S(1)} %copy-done.31), kind=kOutput, calls=%fused_computation.17 | convolution fusion | flops 42301784064 | bytes 59781120 | tf_op jit(solution)/shard_map/nd,nf->df/dot_general | solution.py:90
  466.5 51.1 %convolution_convert_fusion.1 = bf16[1536,8960]{1,0:T(8,128)(2,1)} fusion(bf16[1536,8960]{1,0:T(8,128)(2,1)} %get-tuple-element.50, bf16[1536,1536]{1,0:T(8,128)(2,1)S(1)} %copy-done.7, f32[1536]{0:T(1024)S(1)} %copy-done.29, f32[1536]{0:T(1024)S(1)} %copy-done.31), kind=kOutput, calls=%fused_computation.16 | convolution fusion | flops 42301784064 | bytes 59781120 | tf_op jit(solution)/shard_map/nd,nf->df/dot_general | solution.py:91
  517.6 60.6 %fusion.38 = (bf16[1536]{0:T(1024)(128)(2,1)}, f32[1536]{0:T(1024)S(1)}, f32[1536,1536]{1,0:T(8,128)}) fusion(bf16[1536,1536]{1,0:T(8,128)(2,1)} %copy-done.6, f32[1536]{0:T(1024)S(1)} %copy-done.31, f32[1536]{0:T(1024)S(1)} %copy-done.29, f32[1536,1536]{1,0:T(8,128)} %fusion.117, bf16[1536,8960]{1,0:T(8,128)(2,1)} %get-tuple-element.50, ...), kind=kOutput, calls=%fused_computation.58 | convolution fusion | flops 42297458688 | bytes 78664704 | tf_op jit(solution)/shard_map/nf,df->nd/dot_general | solution.py:93
  670.5 72.5 %bitcast_multiply_fusion.7 = (f32[2,768,2,128]{1,3,2,0:T(8,128)}, f32[2,2,128,768,1]{3,2,4,1,0:T(8,128)}) fusion(f32[2,768,128]{1,2,0:T(8,128)S(1)} %copy-done.4, bf16[2,768,2,6,128]{1,4,3,2,0:T(8,128)(2,1)} %bitcast.212, f32[2,2,768,768,6]{3,2,4,1,0:T(8,128)} %fusion.92, f32[2,2,6,768,768]{3,4,2,1,0:T(8,128)} %get-tuple-element.72, ...), kind=kOutput, calls=%fused_computation.107 | convolution fusion | flops 3723381504 | bytes 121970688 | tf_op jit(solution)/shard_map/bkgqs,bqkgd->bskd/dot_general | solution.py:104
  743.0 71.9 %fusion.12 = f32[2,2,128,6,768]{4,2,3,1,0:T(8,128)} fusion(bf16[2,768,2,128,1]{1,3,4,2,0:T(8,128)(2,1)S(1)} %copy-done.21, f32[2,2,768,768,6]{3,2,4,1,0:T(8,128)} %fusion.92, f32[2,2,6,768,768]{3,4,2,1,0:T(8,128)} %get-tuple-element.72, f32[2,2,6,768]{3,2,1,0:T(8,128)S(1)} %copy-done.34), kind=kOutput, calls=%fused_computation.24 | convolution fusion | flops 3722988288 | bytes 123543552 | tf_op jit(solution)/shard_map/bkgqs,bskd->bqkgd/dot_general | solution.py:103
  814.9 50.7 %reshape.295 = bf16[13762560]{0:T(1024)(128)(2,1)} reshape(bf16[8960,1536]{1,0:T(8,128)(2,1)} %convolution_convert_fusion) | data formatting | bytes 55050240 | tf_op jit(solution)/shard_map/reshape | solution.py:117
  865.6 54.7 %reshape.293 = bf16[13762560]{0:T(1024)(128)(2,1)} reshape(bf16[1536,8960]{1,0:T(8,128)(2,1)} %convolution_convert_fusion.2) | data formatting | bytes 55050240 | tf_op jit(solution)/shard_map/reshape | solution.py:117
  920.3 54.7 %reshape.294 = bf16[13762560]{0:T(1024)(128)(2,1)} reshape(bf16[1536,8960]{1,0:T(8,128)(2,1)} %convolution_convert_fusion.1) | data formatting | bytes 55050240 | tf_op jit(solution)/shard_map/reshape | solution.py:117
  1077.2 72.8 %dynamic-update-slice.2 = bf16[46795776]{0:T(1024)(128)(2,1)} dynamic-update-slice(bf16[46795776]{0:T(1024)(128)(2,1)} %dynamic-update-slice.1, bf16[2359296]{0:T(1024)(128)(2,1)} %reshape.289, s32[]{} %constant.74) | dynamic-update-slice | bytes 9437188
  1176.3 72.7 %dynamic-update-slice.5 = bf16[46795776]{0:T(1024)(128)(2,1)} dynamic-update-slice(bf16[46795776]{0:T(1024)(128)(2,1)} %dynamic-update-slice.4, bf16[2359296]{0:T(1024)(128)(2,1)} %reshape.292, s32[]{} %constant.77) | dynamic-update-slice | bytes 9437188
  1307.3 804.3 %all-reduce.7.cloned.1.call-done = bf16[46795776]{0:T(1024)(128)(2,1)} async-done(((bf16[46795776]{0:T(1024)(128)(2,1)}), bf16[46795776]{0:T(1024)(128)(2,1)}) %all-reduce.7.cloned.1.call-update) | async-done | bytes 93591568
  2118.0 32.1 psum.7
  2150.8 33.9 %fusion.107 = (bf16[2924736]{0:T(1024)(128)(2,1)}, f32[2924736]{0:T(1024)}, f32[2924736]{0:T(1024)}, f32[2924736]{0:T(1024)}) fusion(f32[2924736]{0:T(1024)} %param.27, s32[]{:T(128)S(6)} %mul.344, f32[]{:T(128)S(6)} %mul.334, bf16[46795776]{0:T(1024)(128)(2,1)} %all-reduce.7.cloned.1.call-done, u32[]{:T(128)S(6)} %multiply.41, f32[2924736]{0:T(1024)} %param.28, ...), kind=kLoop, calls=%fused_computation.154 | loop fusion | flops 73118400 | bytes 81892624 | tf_op jit(solution)/shard_map/convert_element_type | solution.py:159
  2213.6 88.9 %dynamic-update-slice = bf16[46795776]{0:T(1024)(128)(2,1)} dynamic-update-slice(bf16[46795776]{0:T(1024)(128)(2,1)} %broadcast.135, bf16[2924736]{0:T(1024)(128)(2,1)} %get-tuple-element.46, u32[]{:T(128)S(6)} %multiply.39) | dynamic-update-slice | bytes 11698948
  2314.5 790.7 %all-reduce.5.cloned.1.call-done = bf16[46795776]{0:T(1024)(128)(2,1)} async-done(((bf16[46795776]{0:T(1024)(128)(2,1)}), bf16[46795776]{0:T(1024)(128)(2,1)}) %all-reduce.5.cloned.1.call-update) | async-done | bytes 93591568
  3105.3 54.0 %fusion.110 = (bf16[13762560]{0:T(1024)(128)(2,1)}, bf16[13762560]{0:T(1024)(128)(2,1)}, bf16[13762560]{0:T(1024)(128)(2,1)}) fusion(bf16[46795776]{0:T(1024)(128)(2,1)} %all-reduce.5.cloned.1.call-done), kind=kLoop, calls=%fused_computation.155 | loop fusion | bytes 165150720 | tf_op jit(solution)/shard_map/slice | solution.py:143
  3159.3 50.2 %slice.111 = bf16[8960,1536]{1,0:T(8,128)(2,1)} reshape(bf16[13762560]{0:T(1024)(128)(2,1)} %get-tuple-element.52) | data formatting | bytes 55050240 | tf_op jit(solution)/shard_map/slice | solution.py:143
  3243.5 47.9 %reshape.298 = bf16[1536,8960]{1,0:T(8,128)(2,1)} reshape(bf16[13762560]{0:T(1024)(128)(2,1)} %get-tuple-element.53) | data formatting | bytes 55050240 | tf_op jit(solution)/shard_map/reshape | solution.py:143
  3291.4 47.9 %reshape.297 = bf16[1536,8960]{1,0:T(8,128)(2,1)} reshape(bf16[13762560]{0:T(1024)(128)(2,1)} %get-tuple-element.54) | data formatting | bytes 55050240 | tf_op jit(solution)/shard_map/reshape | solution.py:143
  (162 shorter events, 485.3 us)
Async XLA Ops:
  7.2 2104.4 %all-reduce.7.cloned.1.call-start = ((), (), s32[]{:S(2)}) async-start(), calls=%async_computation.1 | async-start | bytes 187183104
  21.4 11.3 copy-start.5
  53.8 26.9 copy-start.11
  80.7 22.6 copy-start.33
  103.2 12.9 slice-start
  116.1 12.1 copy-start.8
  116.3 12.0 copy-start.28
  128.2 52.2 %copy-start.6 = (bf16[1536,1536]{1,0:T(8,128)(2,1)}, bf16[1536,1536]{1,0:T(8,128)(2,1)S(1)}, u32[]{:S(2)}) copy-start(bf16[1536,1536]{1,0:T(8,128)(2,1)S(1)} %get-tuple-element.74) | copy-start | bytes 14155780
  128.2 52.1 %copy-start.30 = (f32[1536]{0:T(1024)}, f32[1536]{0:T(1024)S(1)}, u32[]{:S(2)}) copy-start(f32[1536]{0:T(1024)S(1)} %add_rsqrt_fusion) | copy-start | bytes 18436
  362.6 52.4 %copy-start.7 = (bf16[1536,1536]{1,0:T(8,128)(2,1)S(1)}, bf16[1536,1536]{1,0:T(8,128)(2,1)}, u32[]{:S(2)}) copy-start(bf16[1536,1536]{1,0:T(8,128)(2,1)} %copy-done.6) | copy-start | bytes 14155780
  362.6 52.4 %copy-start.29 = (f32[1536]{0:T(1024)S(1)}, f32[1536]{0:T(1024)}, u32[]{:S(2)}) copy-start(f32[1536]{0:T(1024)} %convert_element_type.160) | copy-start | bytes 18436
  362.6 52.4 %copy-start.31 = (f32[1536]{0:T(1024)S(1)}, f32[1536]{0:T(1024)}, u32[]{:S(2)}) copy-start(f32[1536]{0:T(1024)} %copy-done.30) | copy-start | bytes 18436
  578.2 18.0 slice-start.4
  605.9 18.7 copy-start.34
  624.6 23.0 copy-start.12
  647.7 22.9 copy-start.4
  670.5 72.5 %copy-start.21 = (bf16[2,768,2,128,1]{1,3,4,2,0:T(8,128)(2,1)S(1)}, bf16[2,768,2,128,1]{1,3,4,2,0:T(8,128)(2,1)}, u32[]{:S(2)}) copy-start(bf16[2,768,2,128,1]{1,3,4,2,0:T(8,128)(2,1)} %fusion.76) | copy-start | bytes 2359300
  975.0 9.9 copy-start.20
  1028.3 15.2 slice-start.2
  1031.7 11.8 slice-start.3
  1075.7 74.4 %copy-start.15 = (bf16[192,2,8,128]{3,1,2,0:T(2,128)(2,1)S(1)}, bf16[192,2,8,128]{3,1,2,0:T(2,128)(2,1)}, u32[]{:S(2)}) copy-start(bf16[192,2,8,128]{3,1,2,0:T(2,128)(2,1)} %copy.102) | copy-start | bytes 2359300
  1075.7 87.5 %copy-start.14 = (bf16[192,2,8,128]{3,1,2,0:T(2,128)(2,1)S(1)}, bf16[192,2,8,128]{3,1,2,0:T(2,128)(2,1)}, u32[]{:S(2)}) copy-start(bf16[192,2,8,128]{3,1,2,0:T(2,128)(2,1)} %copy.103) | copy-start | bytes 2359300
  1077.2 171.8 %copy-start.32 = (bf16[1536]{0:T(1024)(128)(2,1)S(1)}, bf16[1536]{0:T(1024)(128)(2,1)}, u32[]{:S(2)}) copy-start(bf16[1536]{0:T(1024)(128)(2,1)} %get-tuple-element.42) | copy-start | bytes 9220
  1307.2 1798.1 %all-reduce.5.cloned.1.call-start = ((), (), s32[]{:S(2)}) async-start(), calls=%async_computation | async-start | bytes 187183104
  (19 other events, 117.0 us)
Sparse Core Ops, SparseCore 0:
  1307.3 804.1 all-reduce.6
  2302.7 802.5 all-reduce.4
where the time goes:
time: 3390 us; the launch traced here: 3350 us
  waiting for transfers between devices  1600 us (47%)
  local copies, waits for them, and re-layouts  830 us (24%)
  matrix products  776 us (23%)
  other arithmetic  102 us (3%)
    unnamed x4, waiting for transfers between devices  1600 us
    unnamed x99, local copies, waits for them, and re-layouts  357 us
    reshape x5, local copies, waits for them, and re-layouts, local_grads(): w_grad.astype(jnp.bfloat16).reshape(-1)  180 us
    slice x6, local copies, waits for them, and re-layouts, split_flat(): pieces.append(flat_vec[offset:offset + weight.size].reshape(weight.shape))  126 us
    reshape x3, local copies, waits for them, and re-layouts, split_flat(): pieces.append(flat_vec[offset:offset + weight.size].reshape(weight.shape))  105 us
    dot_general x1, matrix products, local_grads(): jnp.einsum('nd,fd->nf', dy_flat, w_down, preferred_element_type=jnp.float32)  75.4 us
    dot_general x1, matrix products, local_grads(): jnp.einsum('bkgqs,bqkgd->bskd', d_scores, q_rot, preferred_element_type=j...  72.5 us
    dot_general x1, matrix products, local_grads(): jnp.einsum('bkgqs,bskd->bqkgd', d_scores, k_rot, preferred_element_type=j...  71.9 us
  transfers between devices with their start and end apart: 2, of which 2 were waited for; matrix products, arithmetic and copies ran while one was open for 0% of the time, Pallas kernels for 0%

commit v1 on v0

v1 whole, which is shorter than its diff:
```python
import functools

import jax
import jax.numpy as jnp
import numpy as np
from jax import lax
from jax.experimental import pallas as pl
from jax.experimental.pallas import tpu as pltpu
from jax.sharding import PartitionSpec as P

NORM_EPS = 1e-5
ROPE_BASE = 10000.0
LEARN_RATE = 2e-3
BETA_ONE = 0.9
BETA_TWO = 0.95
ADAM_EPS = 1e-8
WEIGHT_DECAY = 0.1
STEP_COUNT = 100
BF = jnp.bfloat16
F32 = jnp.float32
MESH = pl.DeviceIdType.MESH
LANES = 128
SUB = 16
TILE = 256
HALF_LANES = LANES // 2
DIM = 1536
HEADS = 12
KV_HEADS = 2
GROUP = HEADS // KV_HEADS
KV_DIM = KV_HEADS * LANES
QKV_DIM = DIM + 2 * KV_DIM
FFN = 8960
SEQ = 768
TOK = 2 * SEQ
NDEV = 16
HALF = NDEV // 2
BLK = DIM // NDEV
NPARAM = 46795776
SHARD = NPARAM // NDEV
COLS = FFN // LANES
PER = DIM // LANES
ATTN_ROWS = PER * (2 + 2 * DIM) + 2 * KV_HEADS * DIM
SLAB = BLK * COLS
SLOTS = 5
DOWN_ROWS = FFN // NDEV // SLOTS
BLOCK = 22856
WINDOW = 22880
SCALE = LANES**-0.5
LOG2_E = float(np.log2(np.e))
HBM = pl.BlockSpec(memory_space=pl.ANY)

HOLDERS = "1b028a37945dc6fe" + "6745e81d9c0a2fb3" + "23b95c081da7ef46"
SLAB_DEV = [int(c, NDEV) for c in HOLDERS]
ORDER = [[SLAB_DEV[w * NDEV : (w + 1) * NDEV].index(d) for d in range(NDEV)] for w in range(3)]
SAME = list(range(NDEV))

PLAN = {
    "ffn": ("0259bb", "148abb"),
    "wgrad": ("136777",),
    "dn": ("138bdr", "25cegi", "48fhjr", "lmoqrr"),
    "attn_bwd": ("1258ab", "2369bb", "247abb"),
    "dx": ("1245",),
}


def mm(a, b):
    return jnp.dot(a, b, preferred_element_type=F32)


def mm_nt(a, b):
    return lax.dot_general(a, b, (((1,), (1,)), ((), ())), preferred_element_type=F32)


def mm_tn(a, b):
    return lax.dot_general(a, b, (((0,), (0,)), ((), ())), preferred_element_type=F32)


def step(c):
    return int(c, 36)


def once(i):
    return pl.when(i == 0)


def row_mean(x):
    return jnp.mean(x, axis=-1, keepdims=True)


def row_sum(x):
    return jnp.sum(x, axis=-1, keepdims=True)


def inv_rms(x):
    return lax.rsqrt(row_mean(x * x) + NORM_EPS)


def spec(shape, index, first=0):
    return pl.BlockSpec(shape, lambda *g: tuple(0 if c == "." else g["ijk".index(c)] + first for c in index))


def full(shape):
    return pl.BlockSpec(shape, lambda *_: (0,) * len(shape), pipeline_mode=pl.Buffered(1))


def bf(*shapes):
    return [jax.ShapeDtypeStruct(s, BF) for s in shapes]


def f32(*shapes):
    return [jax.ShapeDtypeStruct(s, F32) for s in shapes]


def dma(*shape):
    return pltpu.SemaphoreType.DMA(shape)


def pcall(kernel, *, grid, in_specs, out_specs, out_shape, name, scratch=(), carry=(), cid=None):
    carry = list(carry or ())
    head, skip = len(in_specs), len(carry)

    def body(*refs):
        kernel(*refs[:head], *refs[head + skip :])

    remote = {} if cid is None else dict(collective_id=cid, has_side_effects=True)
    call = pl.pallas_call(
        body,
        grid=grid,
        in_specs=list(in_specs) + [HBM] * skip,
        out_specs=out_specs,
        scratch_shapes=list(scratch),
        out_shape=out_shape,
        input_output_aliases={head + j: j for j in range(skip)},
        compiler_params=pltpu.CompilerParams(vmem_limit_bytes=63 << 20, **remote),
        cost_estimate=pl.CostEstimate(flops=NPARAM * TILE, bytes_accessed=NPARAM, transcendentals=0),
        name=name,
    )
    return lambda *args: call(*args, *carry)


def flat_slabs(d):
    block = SHARD / LANES
    lo = max(0, int((d * block - ATTN_ROWS) // SLAB))
    hi = int(-(-((d + 1) * block - ATTN_ROWS) // SLAB))
    return list(range(lo, min(hi, 3 * NDEV)))


FLAT_SLABS = [flat_slabs(d) for d in range(NDEV)]


def pick(table, me):
    value = jnp.int32(table[0])
    for d in SAME[1:]:
        value = jnp.where(me == d, jnp.int32(table[d]), value)
    return value


AXES = [[(g + s) % 3 for s in range(3)] for g in range(3)]
LOCAL, FINAL, NSEM = range(10, 13)


def remote_copy(src, dst, send, recv, device):
    return pltpu.make_async_remote_copy(src, dst, send, recv, device_id=(device,), device_id_type=MESH)


class Scatter:
    def __init__(self, a, out, bufs, n, width, sq, row0=0):
        self.a, self.out, self.n, self.sq, self.rows = a, out, n, sq, pl.ds(row0, n)
        self.keep, *self.got, self.sems = bufs
        chunks = width // LANES
        ends = [chunks * g // 3 * LANES for g in range(4)]
        self.cols = [pl.ds(lo, hi - lo) for lo, hi in zip(ends, ends[1:])]
        self.me = lax.axis_index("dp")
        self.chip = self.me // 2
        self.bits = [lax.rem(self.chip // (1 << b), 2) for b in range(3)]

    @staticmethod
    def scratch(n, width):
        return [pltpu.VMEM((k, n, width), BF) for k in (HALF, HALF, 4, 2, 1)] + [dma(2, NSEM)]

    def remote(self, src, dst, k, device):
        return remote_copy(src, dst, self.sems.at[0, k], self.sems.at[1, k], device)

    def whole(self, stage, g):
        ref = self.got[stage + 1].at[:, :, self.cols[g]]
        return self.remote(ref, ref, 1 + 3 * stage + g, self.me ^ 1)

    def loads(self):
        for k, dst in enumerate((self.keep, self.got[0])):
            yield pltpu.make_async_copy(self.a[k].at[:, self.rows, :], dst, self.sems.at[k, LOCAL])

    def start(self):
        for copy in self.loads():
            copy.start()

    def block(self, g, stage, t, send):
        axes = AXES[g]
        own = self.bits[axes[stage]]
        j = (1 - own if send else own) * (1 << axes[stage])
        for s in axes[:stage]:
            j += self.bits[s] * (1 << s)
        for r, s in enumerate(axes[stage + 1 :]):
            j += ((t >> r) & 1) * (1 << s)
        return j

    def push(self, stage):
        for g, axes in enumerate(AXES):
            for t in range(4 >> stage):
                src = self.keep.at[self.block(g, stage, t, True), :, self.cols[g]]
                dst = self.got[stage + 1].at[t, :, self.cols[g]]
                self.remote(src, dst, 1 + 3 * stage + g, self.me ^ (2 << axes[stage])).start()

    def sum_rows(self, j, src, cols):
        def body(r, _):
            sl = pl.ds(pl.multiple_of(r * SUB, SUB), SUB)
            self.keep[j, sl, cols] = self.keep[j, sl, cols] + src[sl, cols]
            return 0

        lax.fori_loop(0, self.n // SUB, body, 0)

    def first(self):
        for copy in self.loads():
            copy.wait()

        def body(j, _):
            self.sum_rows(j, self.got[0].at[j], slice(None))
            return 0

        lax.fori_loop(0, HALF, body, 0)
        self.push(0)

    def merge(self, stage):
        for g in range(3):
            self.whole(stage, g).wait_recv()
            for t in range(4 >> stage):
                self.sum_rows(self.block(g, stage, t, False), self.got[stage + 1].at[t], self.cols[g])
        if stage < 2:
            self.push(stage + 1)

    def hand_over(self):
        return pltpu.make_async_copy(self.keep.at[self.chip], self.out, self.sems.at[0, FINAL])

    def last(self):
        self.merge(2)
        self.hand_over().start()

        def body(r, _):
            g = self.keep[self.chip, pl.ds(pl.multiple_of(r * SUB, SUB), SUB), :].astype(F32) * (1.0 / NDEV)
            g = g * g
            total = g[: SUB // 2] + g[SUB // 2 :]
            for c in range(0, total.shape[1], LANES):
                self.sq[:] += total[:, c : c + LANES]
            return 0

        lax.fori_loop(0, self.n // SUB, body, 0)

    def finish(self):
        self.hand_over().wait()
        for stage in range(3):
            for g in range(3):
                self.whole(stage, g).wait_send()

    def run(self, i, at, final=NPARAM):
        stages = (self.start, self.first, *(functools.partial(self.merge, s) for s in range(2)), self.last, self.finish)
        for c, todo in zip(at, stages):
            k = min(step(c), final)
            if isinstance(i, int):
                if i == k:
                    todo()
            else:
                pl.when(i == k)(todo)

    def hand_on(self, sem):
        for k in (1, 2, 4, 8):
            pl.semaphore_signal(sem, inc=1, device_id=(self.me ^ k,), device_id_type=MESH)


class Push:
    def __init__(self, src, got, sems, weight):
        self.src, self.got, self.sems, self.weight = src, got, sems, weight
        self.me = lax.axis_index("dp")

    def each(self):
        held = [self.weight * NDEV + b for b in ORDER[self.weight]]
        for k in range(2):
            own = [([d for d in SAME if h in FLAT_SLABS[d]][k:] or [-1])[0] for h in held]
            slot = [FLAT_SLABS[d].index(h) if d >= 0 else 0 for d, h in zip(own, held)]
            to, slot = pick(own, self.me), pick(slot, self.me)
            dst, recv = self.got.at[slot], self.sems.at[1, slot]
            there = remote_copy(self.src, dst, self.sems.at[0, k], recv, jnp.maximum(to, 0))
            yield to, pltpu.make_async_copy(self.src, dst, recv), there

    def start(self):
        for to, here, there in self.each():
            pl.when(to == self.me)(here.start)
            pl.when((to >= 0) & (to != self.me))(there.start)

    def finish(self):
        for to, _, there in self.each():
            pl.when((to >= 0) & (to != self.me))(there.wait_send)
        for j in range(SLOTS):
            gets = [len(s) > j and s[j] // NDEV == self.weight for s in FLAT_SLABS]
            pl.when(pick(gets, self.me) == 1)(pltpu.make_async_copy(self.src, self.got.at[j], self.sems.at[1, j]).wait)


def push_all(refs, weights, start):
    n = len(weights)
    for j, w in enumerate(weights):
        job = Push(*refs[j::n], w)
        (job.start if start else job.finish)()


SLOT_SEMS = dma(2, SLOTS)


def push_shapes(parts):
    return bf(*((SLOTS, *p.shape) for p, _ in parts))


def push_sems(parts):
    return [SLOT_SEMS] * len(parts)


def greet():
    me = lax.axis_index("dp")
    for k in SAME[1:]:
        pl.semaphore_signal(pltpu.get_barrier_semaphore(), inc=1, device_id=(me ^ k,), device_id_type=MESH)


def met():
    pl.semaphore_wait(pltpu.get_barrier_semaphore(), NDEV - 1)


SQ_SPEC = full((SUB // 2, LANES))
SQ = f32((SUB // 2, LANES))


def blocks(pairs):
    return [g.reshape(HALF, -1, g.shape[-1]) for pair in pairs for g in pair]


def row_block(order, p, core):
    j, mine = 2 * (p % HALF), p // HALF
    return jnp.where(core == mine, order[j + 1], order[j])


def head_pair(w_ref, h):
    return jnp.concatenate([w_ref[h], w_ref[h + 1]], axis=1)


def qkv_kernel(x_ref, g_ref, wq_ref, wk_ref, wv_ref, c_ref, s_ref, nt_ref, q_ref, k_ref, v_ref):
    x = x_ref[:].astype(F32)
    inv = inv_rms(x)
    n = (x * inv * g_ref[:]).astype(BF)
    nt_ref[:] = n.T
    c, s = c_ref[:], s_ref[:]

    def rope(out, t, h):
        for j in range(2):
            u = t[:, j * LANES : (j + 1) * LANES]
            cols = slice((h + j) * LANES, (h + j + 1) * LANES)
            out[:, cols] = (u * c + pltpu.roll(u, HALF_LANES, 1) * s).astype(BF)

    for h in range(0, HEADS, 2):
        rope(q_ref, mm(n, head_pair(wq_ref, h)), h)
    rope(k_ref, mm(n, wk_ref[:]), 0)
    v_ref[:] = mm(n, wv_ref[:]).astype(BF)


def qkv_call(x, gain, wq, wk, wv, cos, sin, tile=TILE):
    r = lambda w: spec((tile, w), "i.")
    return pcall(
        qkv_kernel,
        grid=(TOK // tile,),
        in_specs=[r(DIM), full(gain.shape), full(wq.shape), full(wk.shape), full(wv.shape), r(LANES), r(LANES)],
        out_specs=[spec((DIM, tile), ".i"), r(DIM), r(KV_DIM), r(KV_DIM)],
        out_shape=bf((DIM, TOK), (TOK, DIM), (TOK, KV_DIM), (TOK, KV_DIM)),
        name="qkv",
    )(x, gain, wq, wk, wv, cos, sin)


def probs(q, k, i, bq):
    s = mm_nt(q, k[: (i + 1) * bq])
    r = lax.broadcasted_iota(jnp.int32, (bq, bq), 0)
    c = lax.broadcasted_iota(jnp.int32, (bq, bq), 1)
    d = jnp.where(r >= c, s[:, i * bq :], -1e30)
    s = jnp.concatenate([s[:, : i * bq], d], axis=1) if i else d
    e = jnp.exp2((s - jnp.max(s, axis=-1, keepdims=True)) * (SCALE * LOG2_E))
    return e * (1.0 / row_sum(e))


def head_cols(h):
    return slice(h * LANES, (h + 1) * LANES)


def attn_fwd_kernel(q_ref, k_ref, v_ref, o_ref, ot_ref, *, bq):
    k, v = k_ref[:], v_ref[:]
    for i in range(SEQ // bq):
        r = slice(i * bq, (i + 1) * bq)
        for c in map(head_cols, range(GROUP)):
            p = probs(q_ref[r, c], k, i, bq).astype(BF)
            o = mm(p, v[: (i + 1) * bq]).astype(BF)
            o_ref[r, c] = o
            ot_ref[c, r] = o.T


def attn_fwd(q, k, v, bq=384):
    hq, hk = spec((SEQ, GROUP * LANES), "ij"), spec((SEQ, LANES), "ij")
    return pcall(
        functools.partial(attn_fwd_kernel, bq=bq),
        grid=(TOK // SEQ, KV_HEADS),
        in_specs=[hq, hk, hk],
        out_specs=[hq, spec((GROUP * LANES, SEQ), "ji")],
        out_shape=bf((TOK, DIM), (DIM, TOK)),
        name="attn_fwd",
    )(q, k, v)


def attn_bwd_kernel(q_ref, k_ref, v_ref, do_ref, c_ref, s_ref, out_k, out_r, down_k, down_r, *refs, weights, bq, nh):
    nw = len(weights)
    ins, (dq_ref, dk_ref, dv_ref, out_out, down_a, down_b), refs = refs[:nw], refs[nw:][:6], refs[nw + 6 :]
    gots, (sq, dka, dva), sems, refs = refs[:nw], refs[nw:][:3], refs[nw + 3 :][:nw], refs[2 * nw + 3 :]
    pushes = (*ins, *gots, *sems)
    b, kv, group = (pl.program_id(j) for j in range(3))
    steps = GROUP // nh
    i = (b * KV_HEADS + kv) * steps + group
    n = DOWN_ROWS

    @once(i)
    def _():
        sq[:] = jnp.zeros_like(sq)
        greet()

    @pl.when(i == 1)
    def _():
        met()
        push_all(pushes, weights, True)

    down, plan = (down_k, down_r), PLAN["attn_bwd"]
    Scatter(down, down_a, refs[:6], n, DIM, sq, 3 * n).run(i, plan[0])
    Scatter(down, down_b, refs[6:12], n, DIM, sq, 4 * n).run(i, plan[1])
    Scatter((out_k, out_r), out_out, refs[12:], BLK, DIM, sq).run(i, plan[2])
    pl.when(i == step(plan[0][-1]))(lambda: push_all(pushes, weights, False))
    k, v = k_ref[:], v_ref[:]

    @once(group)
    def _():
        dka[:] = jnp.zeros_like(dka)
        dva[:] = jnp.zeros_like(dva)

    def back(t, c, s):
        return (t * c - pltpu.roll(t, HALF_LANES, 1) * s).astype(BF)

    for i in range(SEQ // bq):
        r, w = slice(i * bq, (i + 1) * bq), (i + 1) * bq
        sides = [[], [], [], []]
        for c in map(head_cols, range(nh)):
            q, do = q_ref[r, c], do_ref[r, c]
            p = probs(q, k, i, bq)
            dp = mm_nt(do, v[:w])
            ds = (p * (dp - row_sum(dp * p)) * SCALE).astype(BF)
            dq_ref[r, c] = back(mm(ds, k[:w]), c_ref[r, :], s_ref[r, :])
            for side, value in zip(sides, (ds, q, p.astype(BF), do)):
                side.append(value)
        ds, q, p, do = (jnp.concatenate(side, axis=0) for side in sides)
        dka[:w, :] += mm_tn(ds, q)
        dva[:w, :] += mm_tn(p, do)

    @pl.when(group == steps - 1)
    def _():
        dk_ref[:] = back(dka[:], c_ref[:], s_ref[:])
        dv_ref[:] = dva[:].astype(BF)


def attn_bwd(q, k, v, do, cos, sin, g_out, g_down, parts, cid, bq=384, nh=2):
    steps = GROUP // nh
    hq = pl.BlockSpec((SEQ, nh * LANES), lambda b, kv, g: (b, kv * steps + g))
    hk = spec((SEQ, LANES), "ij")
    tb = spec((SEQ, LANES), "i.")
    down = (DOWN_ROWS, DIM)
    return pcall(
        functools.partial(attn_bwd_kernel, weights=[w for _, w in parts], bq=bq, nh=nh),
        grid=(TOK // SEQ, KV_HEADS, steps),
        in_specs=[hq, hk, hk, hq, tb, tb] + [HBM] * (4 + len(parts)),
        out_specs=[hq, hk, hk] + [HBM] * (3 + len(parts)) + [SQ_SPEC],
        out_shape=bf((TOK, DIM), k.shape, v.shape, (BLK, DIM), down, down) + push_shapes(parts) + SQ,
        scratch=[pltpu.VMEM((SEQ, LANES), F32)] * 2
        + push_sems(parts)
        + Scatter.scratch(*down) * 2
        + Scatter.scratch(BLK, DIM),
        name="attn_bwd",
        cid=cid,
    )(q, k, v, do, cos, sin, *blocks([g_out, g_down]), *[p for p, _ in parts])


def oproj_kernel(c_ref, wo_ref, x_ref, g_ref, h_ref, n_ref, nt_ref):
    h = (x_ref[:].astype(F32) + mm(c_ref[:], wo_ref[:])).astype(BF)
    h_ref[:] = h
    hw = h.astype(F32)
    inv = inv_rms(hw)
    n = (hw * inv * g_ref[:]).astype(BF)
    n_ref[:] = n
    nt_ref[:] = n.T


def oproj_call(ctx, wo, x, gain, tile=TILE):
    r = spec((tile, DIM), "i.")
    return pcall(
        oproj_kernel,
        grid=(TOK // tile,),
        in_specs=[r, full(wo.shape), r, full(gain.shape)],
        out_specs=[r, r, spec((DIM, tile), ".i")],
        out_shape=bf((TOK, DIM), (TOK, DIM), (DIM, TOK)),
        name="oproj",
    )(ctx, wo, x, gain)


def ffn_kernel(nm_h, dy_h, nt_h, wg_ref, wu_ref, wd_ref, *refs, units, at, weights, count, rc):
    nu, nw = len(units), len(weights)
    ins, refs = refs[: 2 * nu + nw], refs[2 * nu + nw :]
    (gt_ref, dg_ref, du_ref, gg_ref, gu_ref, rg_h, ru_h), refs = refs[:7], refs[7:]
    outs, (sq, nm, dy, na, nb, out, sem, core_sem), refs = refs[: nu + nw], refs[nu + nw :][:8], refs[nu + nw + 8 :]
    pushes = (*ins[2 * nu :], *outs[nu:], *refs[:nw])
    i = pl.program_id(0)
    me = lax.axis_index("dp")
    half, tile = out.shape[-2:]
    loads = [(nm_h, nm), (dy_h, dy), (nt_h, na), (nt_h, nb)]

    @once(i)
    def _():
        sq[:] = jnp.zeros_like(sq)
        for j, (src, dst) in enumerate(loads):
            if src is not nt_h:
                pltpu.make_async_copy(src, dst, sem.at[j]).start()
                continue
            for p in range(NDEV):
                b = row_block(ORDER[j - 2], p, lax.rem(me, 2))
                rows = src.at[pl.ds(pl.multiple_of(b * BLK, BLK), BLK)]
                pltpu.make_async_copy(rows, dst.at[pl.ds(p * BLK, BLK)], sem.at[j]).start()
        greet()

    jobs = [
        Scatter(ins[2 * u :][:2], outs[u], refs[nw + 6 * u :][:6], *unit, sq) for u, unit in enumerate(units)
    ]

    @once(i)
    def _():
        for j, (src, dst) in enumerate(loads):
            pltpu.make_async_copy(src, dst, sem.at[j]).wait()

    slot = lax.rem(i, 2)

    def across(w, dst, t):
        cols = dst.at[:, pl.ds(pl.multiple_of(t * tile, tile), tile)]
        slot = lax.rem(t, 2)
        return remote_copy(out.at[slot, w], cols, core_sem.at[slot, w], core_sem.at[2, w], me ^ 1)

    @pl.when(i >= 2)
    def _():
        for w, dst in enumerate((rg_h, ru_h)):
            across(w, dst, i - 2).wait_send()

    for r in range(0, TOK, rc):
        sl = pl.ds(r, rc)
        gate = mm(nm[sl, :], wg_ref[:])
        up = mm(nm[sl, :], wu_ref[:])
        dga = mm_nt(dy[sl, :], wd_ref[:])
        sig = 1.0 / (1.0 + jnp.exp(-gate))
        act = gate * sig
        gt_ref[:, sl] = (act * up).astype(BF).T
        du_ref[sl, :] = (dga * act).astype(BF)
        dg_ref[sl, :] = (dga * up * sig * (1.0 + gate * (1.0 - sig))).astype(BF)

    @once(i)
    def _():
        met()
        push_all(pushes, weights, True)

    for job, when in zip(jobs, at):
        job.run(i, when, count - 1)
    if nw:
        pl.when(i == count - 1)(lambda: push_all(pushes, weights, False))
    for w, (src, rhs, keep) in enumerate(((na, dg_ref, gg_ref), (nb, du_ref, gu_ref))):
        out[slot, w] = mm(src[:half, :], rhs[:]).astype(BF)
        keep[:] = mm(src[half:, :], rhs[:]).astype(BF)
    for w, dst in enumerate((rg_h, ru_h)):
        across(w, dst, i).start()

        @pl.when(i == count - 1)
        def _(w=w, dst=dst):
            across(w, dst, i - 1).wait_send()
            across(w, dst, i).wait_send()
            remote_copy(dst, dst, core_sem.at[0, w], core_sem.at[2, w], me ^ 1).wait_recv()


def ffn_slice(nm, dy, nt, wg, wu, wd, first, count, prev, arrays, at, parts, cid, tile=TILE, rc=TILE):
    width, half = count * tile, DIM // 2
    units = [(BLK, g.shape[-1]) for g, _ in arrays]
    nmore = len(units) + len(parts)
    col, row, grad = spec((DIM, tile), ".i", first), spec((tile, DIM), "i.", first), spec((half, tile), ".i")
    outs = bf((FFN, TOK), (TOK, FFN), (TOK, FFN), *[(half, width)] * 4, *units)
    return pcall(
        functools.partial(ffn_kernel, units=units, at=at, weights=[w for _, w in parts], count=count, rc=rc),
        grid=(count,),
        in_specs=[HBM] * 3 + [col, col, row] + [HBM] * (nmore + len(units)),
        out_specs=[row, col, col, grad, grad] + [HBM] * (2 + nmore) + [SQ_SPEC],
        out_shape=outs + push_shapes(parts) + SQ,
        scratch=[pltpu.VMEM((TOK, DIM), BF)] * 4
        + [pltpu.VMEM((2, 2, half, tile), BF), dma(4), dma(3, 2)]
        + push_sems(parts)
        + [t for u in units for t in Scatter.scratch(*u)],
        name="ffn",
        carry=prev,
        cid=cid,
    )(nm, dy, nt, wg, wu, wd, *blocks(arrays), *[p for p, _ in parts])


def wgrad_kernel(lhs_h, *refs, cols, nr, per, blk, order, units, at, weights):
    nrhs, nu, nw = len(cols), len(units), len(weights)
    nm = nu + nw
    rhs_h, ins, (keep_h, other_h, *refs) = refs[:nrhs], refs[nrhs:][: nm + nu], refs[nrhs + nm + nu :]
    outs, (sq, *refs) = refs[:nm], refs[nm:]
    me = lax.axis_index("dp")
    rhs, (lhs, out, sem_l, sem_r, sem_o), refs = refs[:nrhs], refs[nrhs:][:5], refs[nrhs + 5 :]
    pushes = (*ins[2 * nu :], *outs[nu:], *refs[:nw])
    size = per * nr
    steps = NDEV * blk // size
    ring = lhs.shape[0]

    def fetch(t):
        for j in range(per):
            p, r = divmod((t * per + j) * nr, blk)
            src = lhs_h.at[pl.ds(pl.multiple_of(row_block(order, p, lax.rem(me, 2)) * blk + r, SUB), nr)]
            pltpu.make_async_copy(src, lhs.at[t % ring, pl.ds(j * nr, nr)], sem_l.at[t % ring]).start()

    def rhs_copy(j):
        c, w = cols[j]
        return pltpu.make_async_copy(rhs_h[j].at[:, pl.ds(c, w)], rhs[j], sem_r.at[j])

    def remote(src, dst, slot):
        return remote_copy(src, dst, sem_o.at[slot], sem_o.at[2], me ^ 1)

    def out_copy(t, wait):
        src, slot, half = out.at[t % 2], t % 2, steps // 2
        if t < half:
            copy = remote(src, other_h.at[pl.ds(t * size, size)], slot)
            (copy.wait_send if wait else copy.start)()
        else:
            copy = pltpu.make_async_copy(src, keep_h.at[pl.ds((t - half) * size, size)], sem_o.at[slot])
            (copy.wait if wait else copy.start)()

    fetch(0)
    for j in range(nrhs):
        rhs_copy(j).start()
    fetch(1)
    sq[:] = jnp.zeros_like(sq)
    greet()
    jobs = [Scatter(ins[2 * u :][:2], outs[u], refs[nw + 6 * u :][:6], *unit, sq) for u, unit in enumerate(units)]
    for t in range(steps):
        if t + 2 < steps:
            fetch(t + 2)
        pltpu.make_async_copy(lhs_h.at[pl.ds(0, size)], lhs.at[t % ring], sem_l.at[t % ring]).wait()
        if t >= 2:
            out_copy(t - 2, True)
        c = 0
        for j in range(nrhs):
            if t == 0:
                rhs_copy(j).wait()
            o = mm(lhs[t % ring], rhs[j][:]).astype(BF)
            out[t % 2, :, c : c + o.shape[1]] = o
            c += o.shape[1]
        if t == 0:
            met()
            push_all(pushes, weights, True)
        out_copy(t, False)
        for job in jobs:
            job.run(t, at)
    for t in range(steps - 2, steps):
        out_copy(t, True)
    remote(other_h, other_h, 0).wait_recv()
    push_all(pushes, weights, False)


def wgrad(lhs_t, rhs, nr, per, order, cid, arrays=(), at="", parts=()):
    rows, width = lhs_t.shape[0], sum(w for _, _, w in rhs)
    units = [(BLK, g.shape[-1]) for g, _ in arrays]
    nmore = len(units) + len(parts)
    return pcall(
        functools.partial(
            wgrad_kernel,
            cols=[r[1:] for r in rhs],
            nr=nr,
            per=per,
            blk=rows // NDEV,
            order=order,
            units=units,
            at=at,
            weights=[w for _, w in parts],
        ),
        grid=(1,),
        in_specs=[HBM] * (1 + len(rhs) + nmore + len(units)),
        out_specs=[HBM] * (2 + nmore) + [SQ_SPEC],
        out_shape=bf(*[(rows // 2, width)] * 2, *units) + push_shapes(parts) + SQ,
        scratch=[pltpu.VMEM((TOK, w), BF) for _, _, w in rhs]
        + [pltpu.VMEM((3, per * nr, TOK), BF), pltpu.VMEM((2, per * nr, width), BF), dma(3), dma(len(rhs)), dma(3)]
        + push_sems(parts)
        + [t for u in units for t in Scatter.scratch(*u)],
        name="wgrad",
        cid=cid,
    )(lhs_t, *[r[0] for r in rhs], *blocks(arrays), *[p for p, _ in parts])


def norm_back(d, x, g_ref, gg_ref):
    inv = inv_rms(x)
    hat = x * inv
    gg_ref[:] += jnp.sum(d * hat, axis=0, keepdims=True)
    dg = d * g_ref[:]
    return inv * (dg - hat * row_mean(dg * hat))


def dn_kernel(dg_ref, du_ref, wg_ref, wu_ref, h_ref, dy_ref, g_ref, up_k, up_r, down_k, down_r, part_h, dh_ref, dl_ref, gg_ref, *refs, up):
    up_out, down_a, down_b, down_c, got, sq, acc, ready, psem, *refs = refs
    push = Push(part_h, got, psem, 0)
    t, k = pl.program_id(0), pl.program_id(1)
    i = t * pl.num_programs(1) + k
    n = DOWN_ROWS

    @once(i)
    def _():
        gg_ref[:] = jnp.zeros_like(gg_ref)
        sq[:] = jnp.zeros_like(sq)
        greet()

    @pl.when(i == 1)
    def _():
        met()
        push.start()

    plan = PLAN["dn"]
    up_h, down_h = (up_k, up_r), (down_k, down_r)
    one = Scatter(down_h, down_a, refs[6:12], n, DIM, sq)
    three = Scatter(down_h, down_c, refs[6:11] + refs[18:], n, DIM, sq, 2 * n)
    Scatter(up_h, up_out, refs[:6], *up, sq).run(i, plan[0])
    one.run(i, plan[1])
    Scatter(down_h, down_b, refs[12:18], n, DIM, sq, n).run(i, plan[2])
    pl.when(i == step(plan[1][-1]))(lambda: one.hand_on(ready))
    pl.when(i == step(plan[3][0]))(lambda: pl.semaphore_wait(ready, 4))
    three.run(i, plan[3])
    pl.when(i == step("r"))(push.finish)

    @once(k)
    def _():
        acc[:] = jnp.zeros_like(acc)

    acc[:] += mm_nt(dg_ref[:], wg_ref[:]) + mm_nt(du_ref[:], wu_ref[:])

    @pl.when(k == pl.num_programs(1) - 1)
    def _():
        def body(r, _):
            sl = pl.ds(pl.multiple_of(r * LANES, LANES), LANES)
            o = norm_back(acc[sl, :], h_ref[sl, :].astype(F32), g_ref, gg_ref) + dy_ref[sl, :].astype(F32)
            dh_ref[sl, :] = o
            dl_ref[sl, :] = o.astype(BF)
            return 0

        lax.fori_loop(0, acc.shape[0] // LANES, body, 0)


def dn_call(dg, du, wg, wu, h, dy, gain, g_up, g_down, part, cid, tt=384, tk=1280):
    up, down = (BLK, g_up[0].shape[-1]), (DOWN_ROWS, DIM)
    act, wgt, row = spec((tt, tk), "ij"), spec((DIM, tk), ".j"), spec((tt, DIM), "i.")
    gained = spec(gain.shape, "..")
    return pcall(
        functools.partial(dn_kernel, up=up),
        grid=(TOK // tt, FFN // tk),
        in_specs=[act, act, wgt, wgt, row, row, full(gain.shape)] + [HBM] * 5,
        out_specs=[row, row, gained] + [HBM] * 5 + [SQ_SPEC],
        out_shape=f32((TOK, DIM)) + bf((TOK, DIM)) + f32(gain.shape) + bf(up, *[down] * 3) + push_shapes([(part, 0)]) + SQ,
        scratch=[pltpu.VMEM((tt, DIM), F32), pltpu.SemaphoreType.REGULAR, SLOT_SEMS]
        + Scatter.scratch(*up)
        + Scatter.scratch(*down) * 2
        + Scatter.scratch(*down)[-1:],
        name="dn",
        cid=cid,
    )(dg, du, wg, wu, h, dy, gain, *blocks([g_up, g_down]), part)


def dx_kernel(
    dq_ref, dk_ref, dv_ref, wq_ref, wk_ref, wv_ref, x_ref, g_ref, dh_ref, sq_ref, g_two_ref, qkv_k, qkv_r,
    dx_ref, gg_ref, qkv_out, told_ref, sq, mine, told, tell, *refs,
):
    i = pl.program_id(0)

    @once(i)
    def _():
        gg_ref[:] = jnp.zeros_like(gg_ref)
        sq[:] = sq_ref[:]
        greet()

    pl.when(i == 1)(met)
    scatter = Scatter((qkv_k, qkv_r), qkv_out, refs, BLK, QKV_DIM, sq)
    scatter.run(i, *PLAN["dx"])
    d = mm_nt(dk_ref[:], wk_ref[:]) + mm_nt(dv_ref[:], wv_ref[:])
    for h in range(0, HEADS, 2):
        d += mm_nt(dq_ref[:, h * LANES : (h + 2) * LANES], head_pair(wq_ref, h))
    dx_ref[:] = (norm_back(d, x_ref[:].astype(F32), g_ref, gg_ref) + dh_ref[:]).astype(BF)

    @pl.when(i == pl.num_programs(0) - 1)
    def _():
        scatter.last()
        for row, ref in enumerate((gg_ref, g_two_ref)):
            for c in range(PER):
                mine[pl.ds(row * PER + c, 1), :] = ref[:, head_cols(c)].astype(BF).astype(F32)
        mine[2 * PER :, :] = sq[:]
        me = lax.axis_index("dp")
        copies = []
        for k in SAME[1:]:
            copies.append(remote_copy(mine, told.at[me], tell.at[0, k], tell.at[1, k], me ^ k))
            copies[-1].start()
        told[me] = mine[:]
        for copy in copies:
            copy.wait()
        told_ref[:] = told[:]
        scatter.finish()


def dx_call(dq, dk, dv, wq, wk, wv, x, gain, dh, squares, g_two, g_qkv, cid, tile=TILE):
    r = lambda w: spec((tile, w), "i.")
    told = (2 * PER + squares.shape[0], LANES)
    return pcall(
        dx_kernel,
        grid=(TOK // tile,),
        in_specs=[r(DIM), r(KV_DIM), r(KV_DIM), full(wq.shape), full(wk.shape), full(wv.shape), r(DIM), full(gain.shape)]
        + [r(DIM), SQ_SPEC, full(gain.shape), HBM, HBM],
        out_specs=[r(DIM), spec(gain.shape, ".."), HBM, full((NDEV, *told))],
        out_shape=bf((TOK, DIM)) + f32(gain.shape) + bf((BLK, QKV_DIM)) + f32((NDEV, *told)),
        scratch=[pltpu.VMEM(squares.shape, F32), pltpu.VMEM(told, F32), pltpu.VMEM((NDEV, *told), F32), dma(2, NDEV)] + Scatter.scratch(BLK, QKV_DIM),
        name="dx",
        cid=cid,
    )(dq, dk, dv, wq, wk, wv, x, gain, dh, squares, g_two, *blocks([g_qkv]))


def to_lane_rows(wide, base, per, part, col, rows):
    for j in range(part.shape[1] // LANES):
        piece = part[:, j * LANES : (j + 1) * LANES].astype(F32)
        wide[pl.ds(base + col + j, rows, stride=per), :] = piece


def attn_flat_kernel(x_ref, o_ref, wide, *, segs):
    base = 0
    for col, per in segs:
        to_lane_rows(wide, base, per, x_ref[:, col * LANES : (col + per) * LANES], 0, BLK)
        base += BLK * per
    o_ref[:] = wide[:].astype(BF)


def attn_flat(x, *segs):
    rows = x.size // LANES
    return pcall(
        functools.partial(attn_flat_kernel, segs=segs),
        grid=(1,),
        in_specs=[full(x.shape)],
        out_specs=full((rows, LANES)),
        out_shape=bf((rows, LANES))[0],
        scratch=[pltpu.VMEM((rows, LANES), F32)],
        name="attn_flat",
    )(x)


def collect_kernel(*refs, ng, nd):
    gates, ups, downs = refs[:ng], refs[ng : 2 * ng], refs[2 * ng : 2 * ng + nd]
    o_h, tall, flat, wide, out, sem = refs[2 * ng + nd :]
    me = lax.axis_index("dp")
    kinds = [[s[k] // NDEV if k < len(s) else -1 for s in FLAT_SLABS] for k in range(SLOTS)]

    def copies(k, parts, dst, axis):
        at = 0
        for p in parts:
            n = p.shape[axis]
            to = dst.at[:, pl.ds(at, n)] if axis == 2 else dst.at[pl.ds(at, n)]
            yield pltpu.make_async_copy(p.at[k], to, sem.at[0])
            at += n

    for k in range(SLOTS):
        kind = pick(kinds[k], me)
        for w, parts in enumerate((gates, ups, downs)):

            @pl.when(kind == w)
            def _(k=k, w=w, parts=parts):
                todo = list(copies(k, parts, *((tall, 1) if w == 2 else (flat, 2))))
                for c in todo:
                    c.start()
                for c in todo:
                    c.wait()

        def store(k=k):
            return pltpu.make_async_copy(out, o_h.at[pl.ds(k * SLAB, SLAB)], sem.at[1])

        @pl.when(kind == 2)
        def _():
            to_lane_rows(wide, 0, PER, tall, 0, tall.shape[0])

        @pl.when((kind == 0) | (kind == 1))
        def _():
            to_lane_rows(wide, 0, COLS, flat, 0, BLK)

        if k:
            store(k - 1).wait()
        out[:] = wide[:].astype(BF)
        store().start()
    store().wait()


def collect(gates, ups, downs):
    parts = [*gates, *ups, *downs]
    return pcall(
        functools.partial(collect_kernel, ng=len(gates), nd=len(downs)),
        grid=(1,),
        in_specs=[HBM] * len(parts),
        out_specs=HBM,
        out_shape=bf((SLOTS * SLAB, LANES))[0],
        scratch=[
            pltpu.VMEM((FFN // NDEV, DIM), BF),
            pltpu.VMEM((BLK, FFN), BF),
            pltpu.VMEM((SLAB, LANES), F32),
            pltpu.VMEM((SLAB, LANES), BF),
            dma(2),
        ],
        name="collect",
    )(*parts)


def paste_kernel(*refs, pieces):
    srcs, (o_ref, sem) = refs[:-2], refs[-2:]
    todo = []
    for s, lead, row, n, dst in pieces:
        src = srcs[s] if lead is None else srcs[s].at[lead]
        todo.append(pltpu.make_async_copy(src.at[pl.ds(row, n)], o_ref.at[pl.ds(dst, n)], sem.at[len(todo)]))
    for c in todo:
        c.start()
    for c in todo:
        c.wait()


def paste(srcs, pieces):
    placed, at = [], 0
    for p in pieces:
        placed.append((*p, at))
        at += p[-1]
    return pcall(
        functools.partial(paste_kernel, pieces=placed),
        grid=(1,),
        in_specs=[HBM] * len(srcs),
        out_specs=full((WINDOW, LANES)),
        out_shape=bf((WINDOW, LANES))[0],
        scratch=[dma(len(placed))],
        name="paste",
    )(*srcs)


def unflat_kernel(x_ref, o_ref, wide, *, per, skew, head_major):
    wide[:] = x_ref[:].astype(F32)
    n = (x_ref.shape[0] - SUB * (skew > 0)) // per
    for j in range(per):
        t = wide[pl.ds(j + skew, n, stride=per), :].astype(BF)
        if head_major:
            o_ref[j] = t
        else:
            o_ref[:, j * LANES : (j + 1) * LANES] = t


def unflat(flat, start, rows, per, tile, head_major=False):
    out = (per, rows, LANES) if head_major else (rows, per * LANES)
    skew = start % 8
    n, window = tile * per, tile * per + SUB * (skew > 0)
    source = lambda i: (pl.multiple_of(start - skew + n * i, 8), 0)
    return pcall(
        functools.partial(unflat_kernel, per=per, skew=skew, head_major=head_major),
        grid=(rows // tile,),
        in_specs=[pl.BlockSpec((pl.Element(window), pl.Element(LANES)), source)],
        out_specs=spec((per, tile, LANES), ".i.") if head_major else spec((tile, per * LANES), "i."),
        out_shape=bf(out)[0],
        scratch=[pltpu.VMEM((window, LANES), F32)],
        name="unflat",
    )(flat)


def rope_tables(positions):
    inv_freq = ROPE_BASE ** (-jnp.arange(HALF_LANES, dtype=F32) / HALF_LANES)
    angles = positions.astype(F32).reshape(-1)[:, None] * inv_freq
    cos, sin = jnp.cos(angles), jnp.sin(angles)
    return jnp.concatenate([cos, cos], axis=-1), jnp.concatenate([-sin, sin], axis=-1)


def adamw_apply(grad_vec, grad_norm, master_vec, mean_vec, var_vec, first_index):
    clip_scale = jnp.minimum(1.0, 1.0 / (grad_norm + 1e-6))
    clipped = grad_vec * clip_scale
    new_mean = BETA_ONE * mean_vec + (1.0 - BETA_ONE) * clipped
    new_var = BETA_TWO * var_vec + (1.0 - BETA_TWO) * clipped * clipped
    mean_hat = new_mean / (1.0 - BETA_ONE**STEP_COUNT)
    var_hat = new_var / (1.0 - BETA_TWO**STEP_COUNT)
    flat_index = first_index + lax.iota(jnp.int32, master_vec.shape[0])
    gain_two = ATTN_ROWS * LANES - DIM
    is_gain = (flat_index < DIM) | ((flat_index >= gain_two) & (flat_index < gain_two + DIM))
    decays = jnp.where(is_gain, 0.0, WEIGHT_DECAY)
    new_master = master_vec - LEARN_RATE * (mean_hat / (jnp.sqrt(var_hat) + ADAM_EPS) + decays * master_vec)
    return new_master, new_mean, new_var


def gradients(x, dy, pos_loc, attn_gain, w_query, w_key, w_value, w_out, mlp_gain, w_gate, w_up, w_down):
    wq, wk, wv, wo = w_query.transpose(1, 0, 2), w_key.reshape(DIM, -1), w_value.reshape(DIM, -1), w_out.reshape(DIM, DIM)
    gain_one, gain_two = attn_gain.astype(F32)[None], mlp_gain.astype(F32)[None]
    cos, sin = rope_tables(pos_loc)
    ids = iter(range(1, NDEV))

    normed_t, q, k, v = qkv_call(x, gain_one, wq, wk, wv, cos, sin)
    ctx, ctx_t = attn_fwd(q, k, v)
    hidden, nm, nm_t = oproj_call(ctx, wo, x, gain_two)

    prev, last, parts, gots, squares = None, [], [], [], []
    tiles = FFN // TILE
    ends = [-(-tiles * s // 3) for s in range(4)]
    for lo, hi, when in zip(ends, ends[1:], ((), PLAN["ffn"], PLAN["ffn"])):
        results = ffn_slice(nm, dy, nm_t, w_gate, w_up, w_down, lo, hi - lo, prev, last, when, parts, next(ids))
        prev, (gate, up, gate_r, up_r, *sums, sq) = results[:3], results[3:]
        gots += sums[2:]
        last, parts = [(gate, gate_r), (up, up_r)], list(zip(sums, range(2)))
        squares.append(sq)
    gated_t, d_gate, d_up = prev
    *g_down, part, got_a, got_b, sq = wgrad(
        gated_t, [(dy, 0, DIM)], DOWN_ROWS, 10, ORDER[2], next(ids), last[:1], *PLAN["wgrad"], parts
    )
    squares.append(sq)
    d_hidden, d_low, g_two, up, *downs, got, sq = dn_call(
        d_gate, d_up, w_gate, w_up, hidden, dy, gain_two, last[1], g_down, part, next(ids)
    )
    gots += [got_a, got_b, got]
    squares.append(sq)
    *g_out, _ = wgrad(ctx_t, [(d_low, 0, DIM)], BLK, 4, SAME, next(ids))
    d_context = mm_nt(d_low, wo).astype(BF)
    parts = [(up, 1)] + [(p, 2) for p in downs]
    d_q, d_k, d_v, out_part, *results, sq = attn_bwd(q, k, v, d_context, cos, sin, g_out, g_down, parts, next(ids))
    gots += results[2:]
    squares.append(sq)
    normed_t, out_slab = lax.optimization_barrier((normed_t, attn_flat(out_part, (0, PER))))
    out_all = lax.all_gather(out_slab, "dp", tiled=True)
    parts = [(p, 2) for p in results[:2]]
    rhs = [(d_q, 0, DIM), (d_k, 0, KV_DIM), (d_v, 0, KV_DIM)]
    *g_qkv, got_a, got_b, _ = wgrad(normed_t, rhs, BLK, 4, SAME, next(ids), parts=parts)
    more = [got_a, got_b]
    g_qkv, out_all = lax.optimization_barrier((g_qkv, out_all))
    gate_a, up_a, gate_b, up_b, gate_c, up_c, *downs = gots + more
    slabs = collect([gate_a, gate_b, gate_c], [up_a, up_b, up_c], downs)
    d_x, _, qkv_part, told = dx_call(
        d_q, d_k, d_v, wq, wk, wv, x, gain_one, d_hidden, sum(squares), g_two, g_qkv, next(ids)
    )
    qkv_all = lax.all_gather(attn_flat(qkv_part, (0, PER), (PER, KV_HEADS), (PER + KV_HEADS, KV_HEADS)), "dp")
    gain_sum = jnp.sum(told[:, : 2 * PER], axis=0).astype(BF)
    gain_mean = gain_sum.astype(F32) / NDEV
    grad_norm = jnp.sqrt(jnp.sum(told[:, 2 * PER :]) + jnp.sum(gain_mean * gain_mean))
    return d_x, grad_norm, gain_sum, qkv_all, out_all, slabs


def flat_block(dev, gain_sum, qkv_all, out_all, slabs):
    qn, kn = BLK * PER, BLK * KV_HEADS
    vn = SUB - PER
    head = jnp.concatenate([jnp.zeros((vn, LANES), BF), gain_sum[:PER]])
    v_at = SUB + NDEV * (qn + kn)
    start = (SHARD // LANES + vn) // SUB * SUB
    split, inside = divmod(start - v_at, kn)

    def first():
        pieces = [(0, None, 0, SUB)]
        pieces += [(1, e, 0, qn) for e in SAME] + [(1, e, qn, kn) for e in SAME]
        pieces += [(1, e, qn + kn, kn) for e in SAME[: (WINDOW - v_at) // kn]]
        return paste([head, qkv_all], pieces)

    def second():
        rear = WINDOW + start - v_at - NDEV * (kn + qn)
        tail = jnp.concatenate([gain_sum[PER:], slabs[: rear - PER]])
        pieces = [(0, split, qn + kn + inside, kn - inside)]
        pieces += [(0, e, qn + kn, kn) for e in SAME[split + 1 :]]
        pieces += [(1, None, 0, NDEV * qn), (2, None, 0, rear)]
        return paste([qkv_all, out_all, tail], pieces)

    away = [d * SHARD - (ATTN_ROWS + SLAB * (s or [0])[0]) * LANES for d, s in enumerate(FLAT_SLABS)]
    rows = [max(0, a) // (SUB * LANES) * SUB for a in away]
    rest = [a - r * LANES for a, r in zip(away, rows)]
    rest[:2] = [vn * LANES, SHARD + (vn - start) * LANES]

    def third():
        return lax.dynamic_slice(slabs, (jnp.asarray(rows, jnp.int32)[dev], 0), (WINDOW, LANES))

    window = lax.switch(jnp.minimum(dev, 2), [first, second, third])
    return lax.dynamic_slice(window.reshape(-1), (jnp.asarray(rest, jnp.int32)[dev],), (SHARD,))


def per_device(x_loc, dy_loc, pos_loc, *args):
    *weights, master_loc, mean_loc, var_loc = args
    dev = lax.axis_index("dp")
    d_x, grad_norm, *sums = gradients(x_loc.reshape(TOK, DIM), dy_loc.reshape(TOK, DIM), pos_loc, *weights)
    grad = flat_block(dev, *sums).astype(F32) / NDEV
    new_master, new_mean, new_var = adamw_apply(grad, grad_norm, master_loc, mean_loc, var_loc, dev * SHARD)

    halo = BLOCK * LANES * NDEV - NPARAM
    edge = lax.ppermute(new_master[:halo], "dp", list(zip(SAME[1:], SAME)))
    shift = BLOCK * LANES - SHARD
    block = lax.dynamic_slice(jnp.concatenate([new_master, edge]), (shift * dev,), (BLOCK * LANES,)).astype(BF)
    flat = lax.all_gather(block.reshape(BLOCK, LANES), "dp", tiled=True)

    new, at = [], 0
    for w in weights:
        rows = w.size // LANES
        if w.shape == (DIM, HEADS, LANES):
            new.append(unflat(flat, at, DIM, HEADS, 256, head_major=True).transpose(1, 0, 2))
        elif w.size >= DIM * DIM:
            per = w.shape[-1] // LANES
            new.append(unflat(flat, at, rows // per, per, {COLS: 192}.get(per, 640 if rows > DIM * PER else 256)).reshape(w.shape))
        else:
            new.append(flat[at : at + rows].reshape(w.shape))
        at += rows
    return (d_x.reshape(x_loc.shape), *new, new_master, new_mean, new_var, grad_norm)


def solution(mesh):
    split, same = P("dp"), P()
    in_specs = (split,) * 3 + (same,) * 9 + (split,) * 3
    out_specs = (split,) + (same,) * 9 + (split,) * 3 + (same,)
    return jax.shard_map(per_device, mesh=mesh, in_specs=in_specs, out_specs=out_specs, check_vma=False)
```

time: 3390 us -> 1360 us (0.40)
  waiting for transfers between devices: 1600 us -> 393 us
  Pallas kernels: 0 us -> 848 us
  local copies, waits for them, and re-layouts: 830 us -> 16.4 us
  matrix products: 776 us -> 12.2 us
  other arithmetic: 102 us -> 55.5 us
    unnamed x4 -> x3, waiting for transfers between devices: 1600 us -> 0.05 us
    pallas_call x0 -> x21, Pallas kernels: none -> 848 us  [pcall(): return lambda *args: call(*args, *carry)]
    dot_general x25 -> x1, matrix products: 749 us -> 12.2 us  [mm_nt(): lax.dot_general(a, b, (((1,), (1,)), ((), ())), preferred_element_type=F32)]
    all_gather x0 -> x3, waiting for transfers between devices: none -> 391 us  [the longest x1 334 us: per_device(): flat = lax.all_gather(block.reshape(BLOCK, LANES), 'dp', tiled=True)]
    unnamed x99 -> x17, local copies, waits for them, and re-layouts: 357 us -> 4.86 us
    reshape x11 -> x2, local copies, waits for them, and re-layouts: 305 us -> 4.05 us  [the longest x1 2.76 us: gradients(): w_value.reshape(DIM, -1)]
    slice x6 -> x3, local copies, waits for them, and re-layouts: 126 us -> 3.73 us  [the longest x1 2.92 us: per_device(): new.append(flat[at:at + rows].reshape(w.shape))]
    convert_element_type x10 -> x1, other arithmetic: 69.5 us -> 0.7 us  [rope_tables(): angles = positions.astype(F32).reshape(-1)[:, None] * inv_freq]
  transfers between devices with their start and end apart: 2 -> 4, of which waited for: 2 -> 4; matrix products, arithmetic and copies ran while one was open for 0% -> 0% of each run, Pallas kernels for 0% -> 3%
where the time goes in v1:
time: 1360 us; the launch traced here: 1350 us
  Pallas kernels  848 us (62%)
  waiting for transfers between devices  393 us (29%)
  other arithmetic  55.5 us (4%)
  between operations  18.9 us (1%)
  local copies, waits for them, and re-layouts  16.4 us (1%)
    pallas_call x21, Pallas kernels, pcall(): return lambda *args: call(*args, *carry)  848 us
    all_gather x1, waiting for transfers between devices, per_device(): flat = lax.all_gather(block.reshape(BLOCK, LANES), 'dp', tiled=True)  334 us
    sub x1, other arithmetic, adamw_apply(): master_vec - LEARN_RATE * (mean_hat / (jnp.sqrt(var_hat) + ADAM_EPS) + de...  32.1 us
    all_gather x1, waiting for transfers between devices, gradients(): lax.all_gather(attn_flat(qkv_part, (0, PER), (PER, KV_HEADS), (PER + KV_H...  29.2 us
    all_gather x1, waiting for transfers between devices, gradients(): out_all = lax.all_gather(out_slab, 'dp', tiled=True)  27.2 us
  transfers between devices with their start and end apart: 4, of which 4 were waited for; matrix products, arithmetic and copies ran while one was open for 0% of the time, Pallas kernels for 3%

profile of v1, /device:TPU:0, one launch (start us, length us, event | category | flops | bytes accessed | tf_op | source)
XLA Modules:
  0.0 1346.2 jit_solution(6367946863676714129)
XLA Ops:
  17.7 16.4 %qkv.1 = (bf16[1536,1536]{1,0:T(8,128)(2,1)}, bf16[1536,1536]{1,0:T(8,128)(2,1)}, bf16[1536,256]{1,0:T(8,128)(2,1)}, bf16[1536,256]{1,0:T(8,128)(2,1)}) custom-call(bf16[1536,1536]{1,0:T(8,128)(2,1)} %bitcast.82, f32[1,1536]{1,0:T(1,128)} %reshape.169.refs_1_.refs_7_, bf16[12,1536,128]{2,1,0:T(8,128)(2,1)} %bitcast.85, ...), custom_call_target="tpu_custom_call" | custom-call | flops 11979718656 | bytes 46795776 | tf_op jit(solution)/shard_map/qkv/pallas_call | solution.py:138
  34.1 23.7 %attn_fwd.1 = (bf16[1536,1536]{1,0:T(8,128)(2,1)}, bf16[1536,1536]{1,0:T(8,128)(2,1)}) custom-call(bf16[1536,1536]{1,0:T(8,128)(2,1)} %get-tuple-element.131.refs_0_, bf16[1536,256]{1,0:T(8,128)(2,1)} %get-tuple-element.132.refs_1_, bf16[1536,256]{1,0:T(8,128)(2,1)} %get-tuple-element.133.refs_2_), custom_call_target="tpu_custom_call" | custom-call | flops 11979718656 | bytes 46795776 | tf_op jit(solution)/shard_map/attn_fwd/pallas_call | solution.py:138
  57.8 14.9 %oproj.1 = (bf16[1536,1536]{1,0:T(8,128)(2,1)}, bf16[1536,1536]{1,0:T(8,128)(2,1)}, bf16[1536,1536]{1,0:T(8,128)(2,1)}) custom-call(bf16[1536,1536]{1,0:T(8,128)(2,1)} %get-tuple-element.134.refs_0_, bf16[1536,1536]{1,0:T(8,128)(2,1)} %bitcast.80, bf16[1536,1536]{1,0:T(8,128)(2,1)} %bitcast.83, f32[1,1536]{1,0:T(1,128)} %reshape.170.refs_3_.refs_6_), custom_call_target="tpu_custom_call" | custom-call | flops 11979718656 | bytes 46795776 | tf_op jit(solution)/shard_map/oproj/pallas_call | solution.py:138
  72.7 92.4 %ffn.3 = (bf16[8960,1536]{1,0:T(8,128)(2,1)}, bf16[1536,8960]{1,0:T(8,128)(2,1)}, bf16[1536,8960]{1,0:T(8,128)(2,1)}, bf16[768,3072]{1,0:T(8,128)(2,1)}, bf16[76...) custom-call(bf16[1536,1536]{1,0:T(8,128)(2,1)} %get-tuple-element.135.refs_0_, ...), custom_call_target="tpu_custom_call" | custom-call | flops 11979718656 | bytes 46795776 | tf_op jit(solution)/shard_map/ffn/pallas_call | solution.py:138
  165.0 98.7 %ffn.4 = (bf16[8960,1536]{1,0:T(8,128)(2,1)}, bf16[1536,8960]{1,0:T(8,128)(2,1)}, bf16[1536,8960]{1,0:T(8,128)(2,1)}, bf16[768,3072]{1,0:T(8,128)(2,1)}, bf16[76...) custom-call(bf16[1536,1536]{1,0:T(8,128)(2,1)} %get-tuple-element.13, ...), custom_call_target="tpu_custom_call", output_to_operand_aliasing={{0}: (10, {}), {1}: (11, {}), {2}: (12, {})} | custom-call | flops 11979718656 | bytes 46795776 | tf_op jit(solution)/shard_map/ffn/pallas_call | solution.py:138
  263.7 106.1 %ffn.5 = (bf16[8960,1536]{1,0:T(8,128)(2,1)}, bf16[1536,8960]{1,0:T(8,128)(2,1)}, bf16[1536,8960]{1,0:T(8,128)(2,1)}, bf16[768,2816]{1,0:T(8,128)(2,1)}, bf16[76...) custom-call(bf16[1536,1536]{1,0:T(8,128)(2,1)} %get-tuple-element.13, ...), custom_call_target="tpu_custom_call", output_to_operand_aliasing={{0}: (12, {}), {1}: (13, {}), {2}: (14, {})} | custom-call | flops 11979718656 | bytes 46795776 | tf_op jit(solution)/shard_map/ffn/pallas_call | solution.py:138
  369.8 65.3 %wgrad.3 = (bf16[4480,1536]{1,0:T(8,128)(2,1)}, bf16[4480,1536]{1,0:T(8,128)(2,1)}, bf16[96,2816]{1,0:T(8,128)(2,1)}, bf16[5,96,3072]{2,1,0:T(8,128)(2,1)}, bf16...) custom-call(bf16[8960,1536]{1,0:T(8,128)(2,1)} %get-tuple-element.158.refs_0_, bf16[1536,1536]{1,0:T(8,128)(2,1)} %bitcast.51, ...), custom_call_target="tpu_custom_call" | custom-call | flops 11979718656 | bytes 46795776 | tf_op jit(solution)/shard_map/wgrad/pallas_call | solution.py:138
  435.1 149.4 %dn.1 = (f32[1536,1536]{1,0:T(8,128)}, bf16[1536,1536]{1,0:T(8,128)(2,1)}, f32[1,1536]{1,0:T(1,128)}, bf16[96,2816]{1,0:T(8,128)(2,1)}, bf16[112,1536]{1,0:T(8,1...) custom-call(bf16[1536,8960]{1,0:T(8,128)(2,1)} %get-tuple-element.15, ...), custom_call_target="tpu_custom_call" | custom-call | flops 11979718656 | bytes 46795776 | tf_op jit(solution)/shard_map/dn/pallas_call | solution.py:138
  584.5 12.2 convolution_convert_fusion.refs_3_
  596.7 13.0 wgrad.4
  609.8 91.1 %attn_bwd.1 = (bf16[1536,1536]{1,0:T(8,128)(2,1)}, bf16[1536,256]{1,0:T(8,128)(2,1)}, bf16[1536,256]{1,0:T(8,128)(2,1)}, bf16[96,1536]{1,0:T(8,128)(2,1)}, bf16[...) custom-call(bf16[1536,1536]{1,0:T(8,128)(2,1)} %get-tuple-element.13, ...), custom_call_target="tpu_custom_call" | custom-call | flops 11979718656 | bytes 46795776 | tf_op jit(solution)/shard_map/attn_bwd/pallas_call | solution.py:138
  703.4 32.4 %wgrad.5 = (bf16[768,2048]{1,0:T(8,128)(2,1)}, bf16[768,2048]{1,0:T(8,128)(2,1)}, bf16[5,112,1536]{2,1,0:T(8,128)(2,1)}, bf16[5,112,1536]{2,1,0:T(8,128)(2,1)}, f32[8,128]{1,0:T(8,128)}) custom-call(bf16[1536,1536]{1,0:T(8,128)(2,1)} %get-tuple-element.187.refs_0_, bf16[1536,1536]{1,0:T(8,128)(2,1)} %get-tuple-element.174.refs_1_.refs_0_, ...), custom_call_target="tpu_custom_call" | custom-call | flops 11979718656 | bytes 46795776 | tf_op jit(solution)/shard_map/wgrad/pallas_call | solution.py:138
  735.8 27.2 %all-gather.5.cloned.1.call-done = bf16[18432,128]{1,0:T(8,128)(2,1)} async-done(((bf16[1152,128]{1,0:T(8,128)(2,1)}), bf16[18432,128]{1,0:T(8,128)(2,1)}) %all-gather.5.cloned.1.call-update) | async-done | bytes 4718608 | tf_op jit(solution)/shard_map/all_gather | solution.py:1046
  763.1 45.8 %dx.1 = (bf16[1536,1536]{1,0:T(8,128)(2,1)}, f32[1,1536]{1,0:T(1,128)}, bf16[96,2048]{1,0:T(8,128)(2,1)}, f32[16,32,128]{2,1,0:T(8,128)}) custom-call(bf16[1536,1536]{1,0:T(8,128)(2,1)} %get-tuple-element.174.refs_1_.refs_0_, bf16[1536,256]{1,0:T(8,128)(2,1)} %get-tuple-element.175.refs_2_.refs_1_, bf16[1536,256]{1,0:T(8,128)(2,1)} %get-tuple-element.176.refs_3_.refs_2_, ...), custom_call_target="tpu_custom_call" | custom-call | flops 11979718656 | bytes 46795776 | tf_op jit(solution)/shard_map/dx/pallas_call | solution.py:138
  810.8 6.8 collect.1
  822.8 29.2 %all-gather.9.cloned.1.call-done = bf16[24576,128]{1,0:T(8,128)(2,1)} async-done(((bf16[1536,128]{1,0:T(8,128)(2,1)}), bf16[24576,128]{1,0:T(8,128)(2,1)}) %all-gather.9.cloned.1.call-update) | async-done | bytes 6291472 | tf_op jit(solution)/shard_map/all_gather | solution.py:1057
  858.1 32.1 %multiply_subtract_fusion = (f32[2924736]{0:T(1024)}, f32[2924736]{0:T(1024)}, f32[2924736]{0:T(1024)}) fusion(f32[2924736]{0:T(1024)} %param.32, s32[]{:T(128)S(6)} %mul.82, f32[]{:T(128)S(6)} %mul.72, bf16[2928640]{0:T(1024)(128)(2,1)} %get-tuple-element.258, s32[]{:T(128)S(6)} %select_n.20, f32[2924736]{0:T(1024)} %param.33, f32[2924736]{0:T(1024)} %param.34), kind=kLoop, calls=%fused_computation.8 | loop fusion | flops 70193664 | bytes 76043152 | tf_op jit(solution)/shard_map/sub | solution.py:1006
  895.4 16.5 %fusion.8 = bf16[22856,128]{1,0:T(8,128)(2,1)} fusion(s32[]{:T(128)S(6)} %select_n.22, bf16[13312]{0:T(1024)(128)(2,1)S(1)} %collective-permute-done, f32[2924736]{0:T(1024)} %get-tuple-element.254), kind=kLoop, calls=%fused_computation.18 | loop fusion | flops 11702272 | bytes 17576708 | tf_op jit(solution)/shard_map/reshape | solution.py:1109
  911.9 334.1 %all-gather.7.cloned.1.call-done.refs_0_ = bf16[365696,128]{1,0:T(8,128)(2,1)} async-done(((bf16[22856,128]{1,0:T(8,128)(2,1)}), bf16[365696,128]{1,0:T(8,128)(2,1)}) %all-gather.7.cloned.1.call-update) | async-done | bytes 93618192 | tf_op jit(solution)/shard_map/all_gather | solution.py:1109
  1246.0 22.3 %unflat.7 = bf16[1536,8960]{1,0:T(8,128)(2,1)} custom-call(bf16[365696,128]{1,0:T(8,128)(2,1)} %all-gather.7.cloned.1.call-done.refs_0_), custom_call_target="tpu_custom_call" | custom-call | flops 11979718656 | bytes 46795776 | tf_op jit(solution)/shard_map/unflat/pallas_call | solution.py:138
  1268.3 22.3 %unflat.8 = bf16[1536,8960]{1,0:T(8,128)(2,1)} custom-call(bf16[365696,128]{1,0:T(8,128)(2,1)} %all-gather.7.cloned.1.call-done.refs_0_), custom_call_target="tpu_custom_call" | custom-call | flops 11979718656 | bytes 46795776 | tf_op jit(solution)/shard_map/unflat/pallas_call | solution.py:138
  1290.7 25.5 %unflat.9 = bf16[8960,1536]{1,0:T(8,128)(2,1)} custom-call(bf16[365696,128]{1,0:T(8,128)(2,1)} %all-gather.7.cloned.1.call-done.refs_0_), custom_call_target="tpu_custom_call" | custom-call | flops 11979718656 | bytes 46795776 | tf_op jit(solution)/shard_map/unflat/pallas_call | solution.py:138
  1316.2 6.4 unflat.5
  1322.6 6.5 unflat.6
  (47 shorter events, 43.0 us)
Async XLA Ops:
  7.2 755.9 %all-gather.5.cloned.1.call-start = ((), (), s32[]{:S(2)}) async-start(), calls=%async_computation | async-start | bytes 5013504 | tf_op jit(solution)/shard_map/all_gather | solution.py:1046
  700.9 1.9 copy-start.1
  700.9 1.9 copy-start.2
  700.9 1.9 copy-start.3
  700.9 1.9 copy-start.4
  700.9 1.9 copy-start.5
  700.9 1.9 copy-start.6
  702.7 149.3 %all-gather.9.cloned.1.call-start = ((), (), s32[]{:S(2)}) async-start(), calls=%async_computation.2 | async-start | bytes 6684672 | tf_op jit(solution)/shard_map/all_gather | solution.py:1057
  810.7 435.3 %all-gather.7.cloned.1.call-start = ((), (), s32[]{:S(2)}) async-start(), calls=%async_computation.1 | async-start | bytes 99469312 | tf_op jit(solution)/shard_map/all_gather | solution.py:1109
  810.8 6.9 copy-start.7
  810.8 9.4 copy-start
  891.0 4.4 collective-permute-start
Sparse Core Ops, SparseCore 0:
  702.8 60.1 all-gather.4
  810.8 41.1 all-gather.8
  912.0 333.9 all-gather.6

commit v2 on v1

--- a/solution.py
+++ b/solution.py
@@ -21,6 +21,8 @@
 MESH = pl.DeviceIdType.MESH
 LANES = 128
 SUB = 16
+ROWS = SUB // 2
+NAXES = 3
 TILE = 256
 HALF_LANES = LANES // 2
 DIM = 1536
@@ -57,8 +59,8 @@
 PLAN = {
     "ffn": ("0259bb", "148abb"),
     "wgrad": ("136777",),
-    "dn": ("138bdr", "25cegi", "48fhjr", "lmoqrr"),
-    "attn_bwd": ("1258ab", "2369bb", "247abb"),
+    "dn": ("14begg", "26fhij", "48imor", "lmoqrr"),
+    "attn_bwd": ("1369bb", "247abb", "258bbb"),
     "dx": ("1245",),
 }
 
@@ -155,7 +157,7 @@
     return value
 
 
-AXES = [[(g + s) % 3 for s in range(3)] for g in range(3)]
+AXES = [[(g + s) % NAXES for s in range(NAXES)] for g in range(NAXES)]
 LOCAL, FINAL, NSEM = range(10, 13)
 
 
@@ -168,11 +170,11 @@
         self.a, self.out, self.n, self.sq, self.rows = a, out, n, sq, pl.ds(row0, n)
         self.keep, *self.got, self.sems = bufs
         chunks = width // LANES
-        ends = [chunks * g // 3 * LANES for g in range(4)]
+        ends = [chunks * g // NAXES * LANES for g in range(4)]
         self.cols = [pl.ds(lo, hi - lo) for lo, hi in zip(ends, ends[1:])]
         self.me = lax.axis_index("dp")
         self.chip = self.me // 2
-        self.bits = [lax.rem(self.chip // (1 << b), 2) for b in range(3)]
+        self.bits = [lax.rem(self.chip // (1 << b), 2) for b in range(NAXES)]
 
     @staticmethod
     def scratch(n, width):
@@ -183,7 +185,7 @@
 
     def whole(self, stage, g):
         ref = self.got[stage + 1].at[:, :, self.cols[g]]
-        return self.remote(ref, ref, 1 + 3 * stage + g, self.me ^ 1)
+        return self.remote(ref, ref, 1 + NAXES * stage + g, self.me ^ 1)
 
     def loads(self):
         for k, dst in enumerate((self.keep, self.got[0])):
@@ -208,7 +210,7 @@
             for t in range(4 >> stage):
                 src = self.keep.at[self.block(g, stage, t, True), :, self.cols[g]]
                 dst = self.got[stage + 1].at[t, :, self.cols[g]]
-                self.remote(src, dst, 1 + 3 * stage + g, self.me ^ (2 << axes[stage])).start()
+                self.remote(src, dst, 1 + NAXES * stage + g, self.me ^ (2 << axes[stage])).start()
 
     def sum_rows(self, j, src, cols):
         def body(r, _):
@@ -230,7 +232,7 @@
         self.push(0)
 
     def merge(self, stage):
-        for g in range(3):
+        for g in range(NAXES):
             self.whole(stage, g).wait_recv()
             for t in range(4 >> stage):
                 self.sum_rows(self.block(g, stage, t, False), self.got[stage + 1].at[t], self.cols[g])
@@ -247,7 +249,7 @@
         def body(r, _):
             g = self.keep[self.chip, pl.ds(pl.multiple_of(r * SUB, SUB), SUB), :].astype(F32) * (1.0 / NDEV)
             g = g * g
-            total = g[: SUB // 2] + g[SUB // 2 :]
+            total = g[: ROWS] + g[ROWS :]
             for c in range(0, total.shape[1], LANES):
                 self.sq[:] += total[:, c : c + LANES]
             return 0
@@ -256,8 +258,8 @@
 
     def finish(self):
         self.hand_over().wait()
-        for stage in range(3):
-            for g in range(3):
+        for stage in range(NAXES):
+            for g in range(NAXES):
                 self.whole(stage, g).wait_send()
 
     def run(self, i, at, final=NPARAM):
@@ -331,8 +333,8 @@
     pl.semaphore_wait(pltpu.get_barrier_semaphore(), NDEV - 1)
 
 
-SQ_SPEC = full((SUB // 2, LANES))
-SQ = f32((SUB // 2, LANES))
+SQ_SPEC = full((ROWS, LANES))
+SQ = f32((ROWS, LANES))
 
 
 def blocks(pairs):
@@ -421,7 +423,7 @@
     ins, (dq_ref, dk_ref, dv_ref, out_out, down_a, down_b), refs = refs[:nw], refs[nw:][:6], refs[nw + 6 :]
     gots, (sq, dka, dva), sems, refs = refs[:nw], refs[nw:][:3], refs[nw + 3 :][:nw], refs[2 * nw + 3 :]
     pushes = (*ins, *gots, *sems)
-    b, kv, group = (pl.program_id(j) for j in range(3))
+    b, kv, group = (pl.program_id(j) for j in range(NAXES))
     steps = GROUP // nh
     i = (b * KV_HEADS + kv) * steps + group
     n = DOWN_ROWS
@@ -431,7 +433,7 @@
         sq[:] = jnp.zeros_like(sq)
         greet()
 
-    @pl.when(i == 1)
+    @pl.when(i == step("1"))
     def _():
         met()
         push_all(pushes, weights, True)
@@ -719,8 +721,8 @@
 
 
 def dn_kernel(dg_ref, du_ref, wg_ref, wu_ref, h_ref, dy_ref, g_ref, up_k, up_r, down_k, down_r, part_h, dh_ref, dl_ref, gg_ref, *refs, up):
-    up_out, down_a, down_b, down_c, got, sq, acc, ready, psem, *refs = refs
-    push = Push(part_h, got, psem, 0)
+    up_out, down_a, down_b, down_c, got, got_up, got_a, sq, acc, ready, psem, usem, asem, *refs = refs
+    push, push_up, push_a = Push(part_h, got, psem, 0), Push(up_out, got_up, usem, 1), Push(down_a, got_a, asem, 2)
     t, k = pl.program_id(0), pl.program_id(1)
     i = t * pl.num_programs(1) + k
     n = DOWN_ROWS
@@ -731,7 +733,7 @@
         sq[:] = jnp.zeros_like(sq)
         greet()
 
-    @pl.when(i == 1)
+    @pl.when(i == step("1"))
     def _():
         met()
         push.start()
@@ -746,7 +748,14 @@
     pl.when(i == step(plan[1][-1]))(lambda: one.hand_on(ready))
     pl.when(i == step(plan[3][0]))(lambda: pl.semaphore_wait(ready, 4))
     three.run(i, plan[3])
-    pl.when(i == step("r"))(push.finish)
+    pl.when(i == step(plan[0][-1]) + 1)(push_up.start)
+    pl.when(i == step(plan[1][-1]) + 1)(push_a.start)
+
+    @pl.when(i == step("r"))
+    def _():
+        for job in (push, push_up, push_a):
+            job.finish()
+
 
     @once(k)
     def _():
@@ -774,9 +783,10 @@
         functools.partial(dn_kernel, up=up),
         grid=(TOK // tt, FFN // tk),
         in_specs=[act, act, wgt, wgt, row, row, full(gain.shape)] + [HBM] * 5,
-        out_specs=[row, row, gained] + [HBM] * 5 + [SQ_SPEC],
-        out_shape=f32((TOK, DIM)) + bf((TOK, DIM)) + f32(gain.shape) + bf(up, *[down] * 3) + push_shapes([(part, 0)]) + SQ,
-        scratch=[pltpu.VMEM((tt, DIM), F32), pltpu.SemaphoreType.REGULAR, SLOT_SEMS]
+        out_specs=[row, row, gained] + [HBM] * 7 + [SQ_SPEC],
+        out_shape=f32((TOK, DIM)) + bf((TOK, DIM)) + f32(gain.shape) + bf(up, *[down] * 3, *[(SLOTS, *t) for t in (part.shape, up, down)]) + SQ,
+        scratch=[pltpu.VMEM((tt, DIM), F32), pltpu.SemaphoreType.REGULAR]
+        + [SLOT_SEMS] * 3
         + Scatter.scratch(*up)
         + Scatter.scratch(*down) * 2
         + Scatter.scratch(*down)[-1:],
@@ -797,7 +807,7 @@
         sq[:] = sq_ref[:]
         greet()
 
-    pl.when(i == 1)(met)
+    pl.when(i == step("1"))(met)
     scatter = Scatter((qkv_k, qkv_r), qkv_out, refs, BLK, QKV_DIM, sq)
     scatter.run(i, *PLAN["dx"])
     d = mm_nt(dk_ref[:], wk_ref[:]) + mm_nt(dv_ref[:], wv_ref[:])
@@ -958,6 +968,68 @@
     )(*srcs)
 
 
+def gather_kernel(x_ref, o_ref, buf, sems, local):
+    me = lax.axis_index("dp")
+    n = BLOCK // (NAXES * ROWS) * ROWS
+    spans = [(0, n), (n, n), (2 * n, BLOCK - 2 * n)]
+    sent = []
+
+    def rows(g, s):
+        e = me
+        for b, axis in enumerate(AXES[g]):
+            if s >> b & 1:
+                e = e ^ (2 << axis)
+        return pl.ds(pl.multiple_of(e * BLOCK + spans[g][0], ROWS), spans[g][1])
+
+    def send(g, s, k):
+        to = me ^ 1 if k == NAXES else me ^ (2 << AXES[g][k])
+        dst = o_ref.at[rows(g, s)]
+        src = dst if s else x_ref.at[pl.ds(*spans[g])]
+        there = s + HALF if k == NAXES else s | 1 << k
+        copy = remote_copy(src, dst, sems.at[0, g, there], sems.at[1, g, there], to)
+        copy.start()
+        sent.append(copy)
+
+    def landed(g, t):
+        ref = o_ref.at[pl.ds(*spans[g])]
+        remote_copy(ref, ref, sems.at[0, g, t], sems.at[1, g, t], me ^ 1).wait_recv()
+
+    into = pltpu.make_async_copy(x_ref, buf, local.at[0])
+    back = pltpu.make_async_copy(buf, o_ref.at[pl.ds(pl.multiple_of(me * BLOCK, ROWS), BLOCK)], local.at[1])
+    into.start()
+    greet()
+    met()
+    for k in range(4):
+        for g in range(NAXES):
+            send(g, 0, k)
+    into.wait()
+    back.start()
+    for t in range(1, HALF):
+        for g in range(NAXES):
+            landed(g, t)
+            for k in range(t.bit_length(), 4):
+                send(g, t, k)
+    for t in range(HALF, NDEV):
+        for g in range(NAXES):
+            landed(g, t)
+    for copy in sent:
+        copy.wait_send()
+    back.wait()
+
+
+def gather(block, cid):
+    return pcall(
+        gather_kernel,
+        grid=(1,),
+        in_specs=[HBM],
+        out_specs=HBM,
+        out_shape=bf((NDEV * BLOCK, LANES))[0],
+        scratch=[pltpu.VMEM((BLOCK, LANES), BF), dma(2, NAXES, NDEV), dma(2)],
+        name="gather",
+        cid=cid,
+    )(block)
+
+
 def unflat_kernel(x_ref, o_ref, wide, *, per, skew, head_major):
     wide[:] = x_ref[:].astype(F32)
     n = (x_ref.shape[0] - SUB * (skew > 0)) // per
@@ -971,9 +1043,9 @@
 
 def unflat(flat, start, rows, per, tile, head_major=False):
     out = (per, rows, LANES) if head_major else (rows, per * LANES)
-    skew = start % 8
+    skew = start % ROWS
     n, window = tile * per, tile * per + SUB * (skew > 0)
-    source = lambda i: (pl.multiple_of(start - skew + n * i, 8), 0)
+    source = lambda i: (pl.multiple_of(start - skew + n * i, ROWS), 0)
     return pcall(
         functools.partial(unflat_kernel, per=per, skew=skew, head_major=head_major),
         grid=(rows // tile,),
@@ -1031,14 +1103,14 @@
         gated_t, [(dy, 0, DIM)], DOWN_ROWS, 10, ORDER[2], next(ids), last[:1], *PLAN["wgrad"], parts
     )
     squares.append(sq)
-    d_hidden, d_low, g_two, up, *downs, got, sq = dn_call(
+    d_hidden, d_low, g_two, _, _, down_b, down_c, *more, sq = dn_call(
         d_gate, d_up, w_gate, w_up, hidden, dy, gain_two, last[1], g_down, part, next(ids)
     )
-    gots += [got_a, got_b, got]
+    gots += [got_a, got_b, *more]
     squares.append(sq)
     *g_out, _ = wgrad(ctx_t, [(d_low, 0, DIM)], BLK, 4, SAME, next(ids))
     d_context = mm_nt(d_low, wo).astype(BF)
-    parts = [(up, 1)] + [(p, 2) for p in downs]
+    parts = [(down_b, 2), (down_c, 2)]
     d_q, d_k, d_v, out_part, *results, sq = attn_bwd(q, k, v, d_context, cos, sin, g_out, g_down, parts, next(ids))
     gots += results[2:]
     squares.append(sq)
@@ -1048,12 +1120,12 @@
     rhs = [(d_q, 0, DIM), (d_k, 0, KV_DIM), (d_v, 0, KV_DIM)]
     *g_qkv, got_a, got_b, _ = wgrad(normed_t, rhs, BLK, 4, SAME, next(ids), parts=parts)
     more = [got_a, got_b]
-    g_qkv, out_all = lax.optimization_barrier((g_qkv, out_all))
     gate_a, up_a, gate_b, up_b, gate_c, up_c, *downs = gots + more
     slabs = collect([gate_a, gate_b, gate_c], [up_a, up_b, up_c], downs)
     d_x, _, qkv_part, told = dx_call(
         d_q, d_k, d_v, wq, wk, wv, x, gain_one, d_hidden, sum(squares), g_two, g_qkv, next(ids)
     )
+    qkv_part, out_all = lax.optimization_barrier((qkv_part, out_all))
     qkv_all = lax.all_gather(attn_flat(qkv_part, (0, PER), (PER, KV_HEADS), (PER + KV_HEADS, KV_HEADS)), "dp")
     gain_sum = jnp.sum(told[:, : 2 * PER], axis=0).astype(BF)
     gain_mean = gain_sum.astype(F32) / NDEV
@@ -1106,7 +1178,7 @@
     edge = lax.ppermute(new_master[:halo], "dp", list(zip(SAME[1:], SAME)))
     shift = BLOCK * LANES - SHARD
     block = lax.dynamic_slice(jnp.concatenate([new_master, edge]), (shift * dev,), (BLOCK * LANES,)).astype(BF)
-    flat = lax.all_gather(block.reshape(BLOCK, LANES), "dp", tiled=True)
+    flat = gather(block.reshape(BLOCK, LANES), NDEV)
 
     new, at = [], 0
     for w in weights:
@@ -1115,7 +1187,7 @@
             new.append(unflat(flat, at, DIM, HEADS, 256, head_major=True).transpose(1, 0, 2))
         elif w.size >= DIM * DIM:
             per = w.shape[-1] // LANES
-            new.append(unflat(flat, at, rows // per, per, {COLS: 192}.get(per, 640 if rows > DIM * PER else 256)).reshape(w.shape))
+            new.append(unflat(flat, at, rows // per, per, {COLS: 384}.get(per, 896 if rows > DIM * PER else 256)).reshape(w.shape))
         else:
             new.append(flat[at : at + rows].reshape(w.shape))
         at += rows

time: 1360 us -> 1300 us (0.956)
  waiting for transfers between devices: 393 us -> 34.1 us
  Pallas kernels: 848 us -> 1150 us
    all_gather x1 -> x0, waiting for transfers between devices: 334 us -> none  [per_device(): flat = lax.all_gather(block.reshape(BLOCK, LANES), 'dp', tiled=True)]
    pallas_call x21 -> x22, Pallas kernels: 848 us -> 1150 us  [pcall(): return lambda *args: call(*args, *carry)]
    all_gather x1, waiting for transfers between devices: 27.2 us -> 0.02 us  [gradients(): out_all = lax.all_gather(out_slab, 'dp', tiled=True)]
  transfers between devices with their start and end apart: 4 -> 3, of which waited for: 4 -> 2; matrix products, arithmetic and copies ran while one was open for 0% -> 0% of each run, Pallas kernels for 3% -> 7%
where the time goes in v2:
time: 1300 us; the launch traced here: 1290 us
  Pallas kernels  1150 us (88%)
  other arithmetic  55.8 us (4%)
  waiting for transfers between devices  34.1 us (3%)
  between operations  19.2 us (1%)
  local copies, waits for them, and re-layouts  16.4 us (1%)
    pallas_call x22, Pallas kernels, pcall(): return lambda *args: call(*args, *carry)  1150 us
    sub x1, other arithmetic, adamw_apply(): master_vec - LEARN_RATE * (mean_hat / (jnp.sqrt(var_hat) + ADAM_EPS) + de...  32.1 us
    all_gather x1, waiting for transfers between devices, gradients(): lax.all_gather(attn_flat(qkv_part, (0, PER), (PER, KV_HEADS), (PER + KV_H...  31 us
  transfers between devices with their start and end apart: 3, of which 2 were waited for; matrix products, arithmetic and copies ran while one was open for 0% of the time, Pallas kernels for 7%

profile of v2, /device:TPU:0, one launch (start us, length us, event | category | flops | bytes accessed | tf_op | source)
XLA Modules:
  0.0 1291.2 jit_solution(13191539294947151204)
XLA Ops:
  17.7 16.4 %qkv.1 = (bf16[1536,1536]{1,0:T(8,128)(2,1)}, bf16[1536,1536]{1,0:T(8,128)(2,1)}, bf16[1536,256]{1,0:T(8,128)(2,1)}, bf16[1536,256]{1,0:T(8,128)(2,1)}) custom-call(bf16[1536,1536]{1,0:T(8,128)(2,1)} %bitcast.82, f32[1,1536]{1,0:T(1,128)} %reshape.169.refs_1_.refs_7_, bf16[12,1536,128]{2,1,0:T(8,128)(2,1)} %bitcast.85, ...), custom_call_target="tpu_custom_call" | custom-call | flops 11979718656 | bytes 46795776 | tf_op jit(solution)/shard_map/qkv/pallas_call | solution.py:140
  34.0 23.7 %attn_fwd.1 = (bf16[1536,1536]{1,0:T(8,128)(2,1)}, bf16[1536,1536]{1,0:T(8,128)(2,1)}) custom-call(bf16[1536,1536]{1,0:T(8,128)(2,1)} %get-tuple-element.128.refs_0_, bf16[1536,256]{1,0:T(8,128)(2,1)} %get-tuple-element.129.refs_1_, bf16[1536,256]{1,0:T(8,128)(2,1)} %get-tuple-element.130.refs_2_), custom_call_target="tpu_custom_call" | custom-call | flops 11979718656 | bytes 46795776 | tf_op jit(solution)/shard_map/attn_fwd/pallas_call | solution.py:140
  57.8 14.9 %oproj.1 = (bf16[1536,1536]{1,0:T(8,128)(2,1)}, bf16[1536,1536]{1,0:T(8,128)(2,1)}, bf16[1536,1536]{1,0:T(8,128)(2,1)}) custom-call(bf16[1536,1536]{1,0:T(8,128)(2,1)} %get-tuple-element.131.refs_0_, bf16[1536,1536]{1,0:T(8,128)(2,1)} %bitcast.80, bf16[1536,1536]{1,0:T(8,128)(2,1)} %bitcast.83, f32[1,1536]{1,0:T(1,128)} %reshape.170.refs_3_.refs_6_), custom_call_target="tpu_custom_call" | custom-call | flops 11979718656 | bytes 46795776 | tf_op jit(solution)/shard_map/oproj/pallas_call | solution.py:140
  72.7 92.4 %ffn.3 = (bf16[8960,1536]{1,0:T(8,128)(2,1)}, bf16[1536,8960]{1,0:T(8,128)(2,1)}, bf16[1536,8960]{1,0:T(8,128)(2,1)}, bf16[768,3072]{1,0:T(8,128)(2,1)}, bf16[76...) custom-call(bf16[1536,1536]{1,0:T(8,128)(2,1)} %get-tuple-element.132.refs_0_, ...), custom_call_target="tpu_custom_call" | custom-call | flops 11979718656 | bytes 46795776 | tf_op jit(solution)/shard_map/ffn/pallas_call | solution.py:140
  165.0 98.6 %ffn.4 = (bf16[8960,1536]{1,0:T(8,128)(2,1)}, bf16[1536,8960]{1,0:T(8,128)(2,1)}, bf16[1536,8960]{1,0:T(8,128)(2,1)}, bf16[768,3072]{1,0:T(8,128)(2,1)}, bf16[76...) custom-call(bf16[1536,1536]{1,0:T(8,128)(2,1)} %get-tuple-element.13, ...), custom_call_target="tpu_custom_call", output_to_operand_aliasing={{0}: (10, {}), {1}: (11, {}), {2}: (12, {})} | custom-call | flops 11979718656 | bytes 46795776 | tf_op jit(solution)/shard_map/ffn/pallas_call | solution.py:140
  263.7 106.1 %ffn.5 = (bf16[8960,1536]{1,0:T(8,128)(2,1)}, bf16[1536,8960]{1,0:T(8,128)(2,1)}, bf16[1536,8960]{1,0:T(8,128)(2,1)}, bf16[768,2816]{1,0:T(8,128)(2,1)}, bf16[76...) custom-call(bf16[1536,1536]{1,0:T(8,128)(2,1)} %get-tuple-element.13, ...), custom_call_target="tpu_custom_call", output_to_operand_aliasing={{0}: (12, {}), {1}: (13, {}), {2}: (14, {})} | custom-call | flops 11979718656 | bytes 46795776 | tf_op jit(solution)/shard_map/ffn/pallas_call | solution.py:140
  369.8 65.3 %wgrad.3 = (bf16[4480,1536]{1,0:T(8,128)(2,1)}, bf16[4480,1536]{1,0:T(8,128)(2,1)}, bf16[96,2816]{1,0:T(8,128)(2,1)}, bf16[5,96,3072]{2,1,0:T(8,128)(2,1)}, bf16...) custom-call(bf16[8960,1536]{1,0:T(8,128)(2,1)} %get-tuple-element.155.refs_0_, bf16[1536,1536]{1,0:T(8,128)(2,1)} %bitcast.51, ...), custom_call_target="tpu_custom_call" | custom-call | flops 11979718656 | bytes 46795776 | tf_op jit(solution)/shard_map/wgrad/pallas_call | solution.py:140
  435.1 146.0 %dn.1 = (f32[1536,1536]{1,0:T(8,128)}, bf16[1536,1536]{1,0:T(8,128)(2,1)}, f32[1,1536]{1,0:T(1,128)}, bf16[96,2816]{1,0:T(8,128)(2,1)}, bf16[112,1536]{1,0:T(8,1...) custom-call(bf16[1536,8960]{1,0:T(8,128)(2,1)} %get-tuple-element.15, ...), custom_call_target="tpu_custom_call" | custom-call | flops 11979718656 | bytes 46795776 | tf_op jit(solution)/shard_map/dn/pallas_call | solution.py:140
  581.1 12.2 convolution_convert_fusion.refs_3_
  593.4 13.0 %wgrad.4 = (bf16[768,1536]{1,0:T(8,128)(2,1)}, bf16[768,1536]{1,0:T(8,128)(2,1)}, f32[8,128]{1,0:T(8,128)}) custom-call(bf16[1536,1536]{1,0:T(8,128)(2,1)} %get-tuple-element.164.refs_0_, bf16[1536,1536]{1,0:T(8,128)(2,1)} %get-tuple-element.163.refs_1_), custom_call_target="tpu_custom_call" | custom-call | flops 11979718656 | bytes 46795776 | tf_op jit(solution)/shard_map/wgrad/pallas_call | solution.py:140
  606.4 85.4 %attn_bwd.1 = (bf16[1536,1536]{1,0:T(8,128)(2,1)}, bf16[1536,256]{1,0:T(8,128)(2,1)}, bf16[1536,256]{1,0:T(8,128)(2,1)}, bf16[96,1536]{1,0:T(8,128)(2,1)}, bf16[...) custom-call(bf16[1536,1536]{1,0:T(8,128)(2,1)} %get-tuple-element.12, ...), custom_call_target="tpu_custom_call" | custom-call | flops 11979718656 | bytes 46795776 | tf_op jit(solution)/shard_map/attn_bwd/pallas_call | solution.py:140
  694.4 23.8 %wgrad.5 = (bf16[768,2048]{1,0:T(8,128)(2,1)}, bf16[768,2048]{1,0:T(8,128)(2,1)}, bf16[5,112,1536]{2,1,0:T(8,128)(2,1)}, bf16[5,112,1536]{2,1,0:T(8,128)(2,1)}, f32[8,128]{1,0:T(8,128)}) custom-call(bf16[1536,1536]{1,0:T(8,128)(2,1)} %get-tuple-element.182.refs_0_, bf16[1536,1536]{1,0:T(8,128)(2,1)} %get-tuple-element.169.refs_1_.refs_0_, ...), custom_call_target="tpu_custom_call" | custom-call | flops 11979718656 | bytes 46795776 | tf_op jit(solution)/shard_map/wgrad/pallas_call | solution.py:140
  718.2 61.3 %dx.1 = (bf16[1536,1536]{1,0:T(8,128)(2,1)}, f32[1,1536]{1,0:T(1,128)}, bf16[96,2048]{1,0:T(8,128)(2,1)}, f32[16,32,128]{2,1,0:T(8,128)}) custom-call(bf16[1536,1536]{1,0:T(8,128)(2,1)} %get-tuple-element.169.refs_1_.refs_0_, bf16[1536,256]{1,0:T(8,128)(2,1)} %get-tuple-element.170.refs_2_.refs_1_, bf16[1536,256]{1,0:T(8,128)(2,1)} %get-tuple-element.171.refs_3_.refs_2_, ...), custom_call_target="tpu_custom_call" | custom-call | flops 11979718656 | bytes 46795776 | tf_op jit(solution)/shard_map/dx/pallas_call | solution.py:140
  781.4 6.8 collect.1
  793.4 31.0 %all-gather.6.cloned.1.call-done = bf16[24576,128]{1,0:T(8,128)(2,1)} async-done(((bf16[1536,128]{1,0:T(8,128)(2,1)}), bf16[24576,128]{1,0:T(8,128)(2,1)}) %all-gather.6.cloned.1.call-update) | async-done | bytes 6291472 | tf_op jit(solution)/shard_map/all_gather | solution.py:1129
  824.4 6.1 conditional.1
  830.5 32.1 %multiply_subtract_fusion = (f32[2924736]{0:T(1024)}, f32[2924736]{0:T(1024)}, f32[2924736]{0:T(1024)}) fusion(f32[2924736]{0:T(1024)} %param.32, s32[]{:T(128)S(6)} %mul.82, f32[]{:T(128)S(6)} %mul.72, bf16[2928640]{0:T(1024)(128)(2,1)} %get-tuple-element.252, s32[]{:T(128)S(6)} %select_n.20, f32[2924736]{0:T(1024)} %param.33, f32[2924736]{0:T(1024)} %param.34), kind=kLoop, calls=%fused_computation.8 | loop fusion | flops 70193664 | bytes 76043152 | tf_op jit(solution)/shard_map/sub | solution.py:1078
  867.8 16.7 %fusion.8.refs_0_ = bf16[22856,128]{1,0:T(8,128)(2,1)} fusion(s32[]{:T(128)S(6)} %select_n.22, bf16[13312]{0:T(1024)(128)(2,1)S(1)} %collective-permute-done, f32[2924736]{0:T(1024)} %get-tuple-element.248), kind=kLoop, calls=%fused_computation.18 | loop fusion | flops 11702272 | bytes 17576708 | tf_op jit(solution)/shard_map/reshape | solution.py:1181
  884.5 313.0 %gather.1.refs_0_ = bf16[365696,128]{1,0:T(8,128)(2,1)} custom-call(bf16[22856,128]{1,0:T(8,128)(2,1)} %fusion.8.refs_0_), custom_call_target="tpu_custom_call" | custom-call | flops 11979718656 | bytes 46795776 | tf_op jit(solution)/shard_map/gather/pallas_call | solution.py:140
  1197.5 20.0 %unflat.7 = bf16[1536,8960]{1,0:T(8,128)(2,1)} custom-call(bf16[365696,128]{1,0:T(8,128)(2,1)} %gather.1.refs_0_), custom_call_target="tpu_custom_call" | custom-call | flops 11979718656 | bytes 46795776 | tf_op jit(solution)/shard_map/unflat/pallas_call | solution.py:140
  1217.4 19.9 %unflat.8 = bf16[1536,8960]{1,0:T(8,128)(2,1)} custom-call(bf16[365696,128]{1,0:T(8,128)(2,1)} %gather.1.refs_0_), custom_call_target="tpu_custom_call" | custom-call | flops 11979718656 | bytes 46795776 | tf_op jit(solution)/shard_map/unflat/pallas_call | solution.py:140
  1237.4 23.5 %unflat.9 = bf16[8960,1536]{1,0:T(8,128)(2,1)} custom-call(bf16[365696,128]{1,0:T(8,128)(2,1)} %gather.1.refs_0_), custom_call_target="tpu_custom_call" | custom-call | flops 11979718656 | bytes 46795776 | tf_op jit(solution)/shard_map/unflat/pallas_call | solution.py:140
  1260.9 6.4 unflat.5
  1267.3 6.5 unflat.6
  (45 shorter events, 36.9 us)
Async XLA Ops:
  7.2 772.3 %all-gather.4.cloned.1.call-start = ((), (), s32[]{:S(2)}) async-start(), calls=%async_computation | async-start | bytes 5013504 | tf_op jit(solution)/shard_map/all_gather | solution.py:1118
  691.9 1.9 copy-start.1
  691.9 1.9 copy-start.2
  691.9 1.9 copy-start.3
  691.9 1.9 copy-start.4
  691.9 1.9 copy-start.5
  691.9 1.9 copy-start.6
  693.7 130.7 %all-gather.6.cloned.1.call-start = ((), (), s32[]{:S(2)}) async-start(), calls=%async_computation.1 | async-start | bytes 6684672 | tf_op jit(solution)/shard_map/all_gather | solution.py:1129
  781.4 6.9 copy-start
  781.4 9.5 copy-start.7
  863.4 4.4 collective-permute-start
Sparse Core Ops, SparseCore 0:
  693.8 57.9 all-gather.3
  781.5 42.8 all-gather.5

commit v3 on v2

--- a/solution.py
+++ b/solution.py
@@ -57,7 +57,7 @@
 SAME = list(range(NDEV))
 
 PLAN = {
-    "ffn": ("0259bb", "148abb"),
+    "ffn": ("0369bb", "158abb"),
     "wgrad": ("136777",),
     "dn": ("14begg", "26fhij", "48imor", "lmoqrr"),
     "attn_bwd": ("1369bb", "247abb", "258bbb"),
@@ -1184,10 +1184,10 @@
     for w in weights:
         rows = w.size // LANES
         if w.shape == (DIM, HEADS, LANES):
-            new.append(unflat(flat, at, DIM, HEADS, 256, head_major=True).transpose(1, 0, 2))
+            new.append(unflat(flat, at, DIM, HEADS, 512, head_major=True).transpose(1, 0, 2))
         elif w.size >= DIM * DIM:
             per = w.shape[-1] // LANES
-            new.append(unflat(flat, at, rows // per, per, {COLS: 384}.get(per, 896 if rows > DIM * PER else 256)).reshape(w.shape))
+            new.append(unflat(flat, at, rows // per, per, {COLS: 384}.get(per, 896 if rows > DIM * PER else 512)).reshape(w.shape))
         else:
             new.append(flat[at : at + rows].reshape(w.shape))
         at += rows

time: 1300 us -> 1300 us (level)
  no operation moved by 1% of the time
where the time goes in v3:
time: 1300 us; the launch traced here: 1290 us
  Pallas kernels  1160 us (89%)
  other arithmetic  55.8 us (4%)
  waiting for transfers between devices  34.1 us (3%)
  between operations  19.2 us (1%)
  local copies, waits for them, and re-layouts  16.4 us (1%)
    pallas_call x22, Pallas kernels, pcall(): return lambda *args: call(*args, *carry)  1160 us
    sub x1, other arithmetic, adamw_apply(): master_vec - LEARN_RATE * (mean_hat / (jnp.sqrt(var_hat) + ADAM_EPS) + de...  32.1 us
    all_gather x1, waiting for transfers between devices, gradients(): lax.all_gather(attn_flat(qkv_part, (0, PER), (PER, KV_HEADS), (PER + KV_H...  31 us
  transfers between devices with their start and end apart: 3, of which 2 were waited for; matrix products, arithmetic and copies ran while one was open for 0% of the time, Pallas kernels for 7%

profile of v3, /device:TPU:0, one launch (start us, length us, event | category | flops | bytes accessed | tf_op | source)
XLA Modules:
  0.0 1294.3 jit_solution(6014770060911874004)
XLA Ops:
  17.7 16.4 %qkv.1 = (bf16[1536,1536]{1,0:T(8,128)(2,1)}, bf16[1536,1536]{1,0:T(8,128)(2,1)}, bf16[1536,256]{1,0:T(8,128)(2,1)}, bf16[1536,256]{1,0:T(8,128)(2,1)}) custom-call(bf16[1536,1536]{1,0:T(8,128)(2,1)} %bitcast.82, f32[1,1536]{1,0:T(1,128)} %reshape.169.refs_1_.refs_7_, bf16[12,1536,128]{2,1,0:T(8,128)(2,1)} %bitcast.85, ...), custom_call_target="tpu_custom_call" | custom-call | flops 11979718656 | bytes 46795776 | tf_op jit(solution)/shard_map/qkv/pallas_call | solution.py:140
  34.0 23.7 %attn_fwd.1 = (bf16[1536,1536]{1,0:T(8,128)(2,1)}, bf16[1536,1536]{1,0:T(8,128)(2,1)}) custom-call(bf16[1536,1536]{1,0:T(8,128)(2,1)} %get-tuple-element.128.refs_0_, bf16[1536,256]{1,0:T(8,128)(2,1)} %get-tuple-element.129.refs_1_, bf16[1536,256]{1,0:T(8,128)(2,1)} %get-tuple-element.130.refs_2_), custom_call_target="tpu_custom_call" | custom-call | flops 11979718656 | bytes 46795776 | tf_op jit(solution)/shard_map/attn_fwd/pallas_call | solution.py:140
  57.8 14.9 %oproj.1 = (bf16[1536,1536]{1,0:T(8,128)(2,1)}, bf16[1536,1536]{1,0:T(8,128)(2,1)}, bf16[1536,1536]{1,0:T(8,128)(2,1)}) custom-call(bf16[1536,1536]{1,0:T(8,128)(2,1)} %get-tuple-element.131.refs_0_, bf16[1536,1536]{1,0:T(8,128)(2,1)} %bitcast.80, bf16[1536,1536]{1,0:T(8,128)(2,1)} %bitcast.83, f32[1,1536]{1,0:T(1,128)} %reshape.170.refs_3_.refs_6_), custom_call_target="tpu_custom_call" | custom-call | flops 11979718656 | bytes 46795776 | tf_op jit(solution)/shard_map/oproj/pallas_call | solution.py:140
  72.7 92.4 %ffn.3 = (bf16[8960,1536]{1,0:T(8,128)(2,1)}, bf16[1536,8960]{1,0:T(8,128)(2,1)}, bf16[1536,8960]{1,0:T(8,128)(2,1)}, bf16[768,3072]{1,0:T(8,128)(2,1)}, bf16[76...) custom-call(bf16[1536,1536]{1,0:T(8,128)(2,1)} %get-tuple-element.132.refs_0_, ...), custom_call_target="tpu_custom_call" | custom-call | flops 11979718656 | bytes 46795776 | tf_op jit(solution)/shard_map/ffn/pallas_call | solution.py:140
  165.0 104.2 %ffn.4 = (bf16[8960,1536]{1,0:T(8,128)(2,1)}, bf16[1536,8960]{1,0:T(8,128)(2,1)}, bf16[1536,8960]{1,0:T(8,128)(2,1)}, bf16[768,3072]{1,0:T(8,128)(2,1)}, bf16[76...) custom-call(bf16[1536,1536]{1,0:T(8,128)(2,1)} %get-tuple-element.13, ...), custom_call_target="tpu_custom_call", output_to_operand_aliasing={{0}: (10, {}), {1}: (11, {}), {2}: (12, {})} | custom-call | flops 11979718656 | bytes 46795776 | tf_op jit(solution)/shard_map/ffn/pallas_call | solution.py:140
  269.3 106.7 %ffn.5 = (bf16[8960,1536]{1,0:T(8,128)(2,1)}, bf16[1536,8960]{1,0:T(8,128)(2,1)}, bf16[1536,8960]{1,0:T(8,128)(2,1)}, bf16[768,2816]{1,0:T(8,128)(2,1)}, bf16[76...) custom-call(bf16[1536,1536]{1,0:T(8,128)(2,1)} %get-tuple-element.13, ...), custom_call_target="tpu_custom_call", output_to_operand_aliasing={{0}: (12, {}), {1}: (13, {}), {2}: (14, {})} | custom-call | flops 11979718656 | bytes 46795776 | tf_op jit(solution)/shard_map/ffn/pallas_call | solution.py:140
  375.9 64.2 %wgrad.3 = (bf16[4480,1536]{1,0:T(8,128)(2,1)}, bf16[4480,1536]{1,0:T(8,128)(2,1)}, bf16[96,2816]{1,0:T(8,128)(2,1)}, bf16[5,96,3072]{2,1,0:T(8,128)(2,1)}, bf16...) custom-call(bf16[8960,1536]{1,0:T(8,128)(2,1)} %get-tuple-element.155.refs_0_, bf16[1536,1536]{1,0:T(8,128)(2,1)} %bitcast.51, ...), custom_call_target="tpu_custom_call" | custom-call | flops 11979718656 | bytes 46795776 | tf_op jit(solution)/shard_map/wgrad/pallas_call | solution.py:140
  440.2 145.3 %dn.1 = (f32[1536,1536]{1,0:T(8,128)}, bf16[1536,1536]{1,0:T(8,128)(2,1)}, f32[1,1536]{1,0:T(1,128)}, bf16[96,2816]{1,0:T(8,128)(2,1)}, bf16[112,1536]{1,0:T(8,1...) custom-call(bf16[1536,8960]{1,0:T(8,128)(2,1)} %get-tuple-element.15, ...), custom_call_target="tpu_custom_call" | custom-call | flops 11979718656 | bytes 46795776 | tf_op jit(solution)/shard_map/dn/pallas_call | solution.py:140
  585.4 12.2 convolution_convert_fusion.refs_3_
  597.7 13.0 %wgrad.4 = (bf16[768,1536]{1,0:T(8,128)(2,1)}, bf16[768,1536]{1,0:T(8,128)(2,1)}, f32[8,128]{1,0:T(8,128)}) custom-call(bf16[1536,1536]{1,0:T(8,128)(2,1)} %get-tuple-element.164.refs_0_, bf16[1536,1536]{1,0:T(8,128)(2,1)} %get-tuple-element.163.refs_1_), custom_call_target="tpu_custom_call" | custom-call | flops 11979718656 | bytes 46795776 | tf_op jit(solution)/shard_map/wgrad/pallas_call | solution.py:140
  610.7 85.1 %attn_bwd.1 = (bf16[1536,1536]{1,0:T(8,128)(2,1)}, bf16[1536,256]{1,0:T(8,128)(2,1)}, bf16[1536,256]{1,0:T(8,128)(2,1)}, bf16[96,1536]{1,0:T(8,128)(2,1)}, bf16[...) custom-call(bf16[1536,1536]{1,0:T(8,128)(2,1)} %get-tuple-element.12, ...), custom_call_target="tpu_custom_call" | custom-call | flops 11979718656 | bytes 46795776 | tf_op jit(solution)/shard_map/attn_bwd/pallas_call | solution.py:140
  698.4 23.8 %wgrad.5 = (bf16[768,2048]{1,0:T(8,128)(2,1)}, bf16[768,2048]{1,0:T(8,128)(2,1)}, bf16[5,112,1536]{2,1,0:T(8,128)(2,1)}, bf16[5,112,1536]{2,1,0:T(8,128)(2,1)}, f32[8,128]{1,0:T(8,128)}) custom-call(bf16[1536,1536]{1,0:T(8,128)(2,1)} %get-tuple-element.182.refs_0_, bf16[1536,1536]{1,0:T(8,128)(2,1)} %get-tuple-element.169.refs_1_.refs_0_, ...), custom_call_target="tpu_custom_call" | custom-call | flops 11979718656 | bytes 46795776 | tf_op jit(solution)/shard_map/wgrad/pallas_call | solution.py:140
  722.1 61.3 %dx.1 = (bf16[1536,1536]{1,0:T(8,128)(2,1)}, f32[1,1536]{1,0:T(1,128)}, bf16[96,2048]{1,0:T(8,128)(2,1)}, f32[16,32,128]{2,1,0:T(8,128)}) custom-call(bf16[1536,1536]{1,0:T(8,128)(2,1)} %get-tuple-element.169.refs_1_.refs_0_, bf16[1536,256]{1,0:T(8,128)(2,1)} %get-tuple-element.170.refs_2_.refs_1_, bf16[1536,256]{1,0:T(8,128)(2,1)} %get-tuple-element.171.refs_3_.refs_2_, ...), custom_call_target="tpu_custom_call" | custom-call | flops 11979718656 | bytes 46795776 | tf_op jit(solution)/shard_map/dx/pallas_call | solution.py:140
  785.4 6.8 collect.1
  797.4 31.0 %all-gather.6.cloned.1.call-done = bf16[24576,128]{1,0:T(8,128)(2,1)} async-done(((bf16[1536,128]{1,0:T(8,128)(2,1)}), bf16[24576,128]{1,0:T(8,128)(2,1)}) %all-gather.6.cloned.1.call-update) | async-done | bytes 6291472 | tf_op jit(solution)/shard_map/all_gather | solution.py:1129
  828.3 6.1 conditional.1
  834.4 32.1 %multiply_subtract_fusion = (f32[2924736]{0:T(1024)}, f32[2924736]{0:T(1024)}, f32[2924736]{0:T(1024)}) fusion(f32[2924736]{0:T(1024)} %param.32, s32[]{:T(128)S(6)} %mul.82, f32[]{:T(128)S(6)} %mul.72, bf16[2928640]{0:T(1024)(128)(2,1)} %get-tuple-element.252, s32[]{:T(128)S(6)} %select_n.20, f32[2924736]{0:T(1024)} %param.33, f32[2924736]{0:T(1024)} %param.34), kind=kLoop, calls=%fused_computation.8 | loop fusion | flops 70193664 | bytes 76043152 | tf_op jit(solution)/shard_map/sub | solution.py:1078
  871.7 16.7 %fusion.8.refs_0_ = bf16[22856,128]{1,0:T(8,128)(2,1)} fusion(s32[]{:T(128)S(6)} %select_n.22, bf16[13312]{0:T(1024)(128)(2,1)S(1)} %collective-permute-done, f32[2924736]{0:T(1024)} %get-tuple-element.248), kind=kLoop, calls=%fused_computation.18 | loop fusion | flops 11702272 | bytes 17576708 | tf_op jit(solution)/shard_map/reshape | solution.py:1181
  888.4 313.0 %gather.1.refs_0_ = bf16[365696,128]{1,0:T(8,128)(2,1)} custom-call(bf16[22856,128]{1,0:T(8,128)(2,1)} %fusion.8.refs_0_), custom_call_target="tpu_custom_call" | custom-call | flops 11979718656 | bytes 46795776 | tf_op jit(solution)/shard_map/gather/pallas_call | solution.py:140
  1201.5 20.0 %unflat.7 = bf16[1536,8960]{1,0:T(8,128)(2,1)} custom-call(bf16[365696,128]{1,0:T(8,128)(2,1)} %gather.1.refs_0_), custom_call_target="tpu_custom_call" | custom-call | flops 11979718656 | bytes 46795776 | tf_op jit(solution)/shard_map/unflat/pallas_call | solution.py:140
  1221.4 19.9 %unflat.8 = bf16[1536,8960]{1,0:T(8,128)(2,1)} custom-call(bf16[365696,128]{1,0:T(8,128)(2,1)} %gather.1.refs_0_), custom_call_target="tpu_custom_call" | custom-call | flops 11979718656 | bytes 46795776 | tf_op jit(solution)/shard_map/unflat/pallas_call | solution.py:140
  1241.3 23.5 %unflat.9 = bf16[8960,1536]{1,0:T(8,128)(2,1)} custom-call(bf16[365696,128]{1,0:T(8,128)(2,1)} %gather.1.refs_0_), custom_call_target="tpu_custom_call" | custom-call | flops 11979718656 | bytes 46795776 | tf_op jit(solution)/shard_map/unflat/pallas_call | solution.py:140
  1264.9 5.9 unflat.5
  1270.8 6.1 unflat.6
  (45 shorter events, 36.9 us)
Async XLA Ops:
  7.2 776.3 %all-gather.4.cloned.1.call-start = ((), (), s32[]{:S(2)}) async-start(), calls=%async_computation | async-start | bytes 5013504 | tf_op jit(solution)/shard_map/all_gather | solution.py:1118
  695.8 1.9 copy-start.1
  695.8 1.9 copy-start.2
  695.8 1.9 copy-start.3
  695.9 1.9 copy-start.4
  695.9 1.9 copy-start.5
  695.9 1.9 copy-start.6
  697.7 130.7 %all-gather.6.cloned.1.call-start = ((), (), s32[]{:S(2)}) async-start(), calls=%async_computation.1 | async-start | bytes 6684672 | tf_op jit(solution)/shard_map/all_gather | solution.py:1129
  785.3 6.9 copy-start
  785.3 9.5 copy-start.7
  867.3 4.4 collective-permute-start
Sparse Core Ops, SparseCore 0:
  697.8 57.9 all-gather.3
  785.5 42.8 all-gather.5
